TPU v7x, 32 devices: a whole 2x2x4 slice. The times are simulated.
32 devices in a mesh: gx: 4 (over y, x), gy: 4 (over z), gz: 2 (over core).
Axes of the slice: x: 2, y: 2, z: 4, core: 2. Of those that a mesh axis runs over, the one named last changes fastest.
Arguments:
- load: float32 [256, 256, 256], P('gx', 'gy', 'gz'), may hold values from -12 to 12
- stiffness: float32 [256, 256, 256], P('gx', 'gy', 'gz'), may hold values from 0.02 to 2
- prestress: float32 [256, 256], P(('gx', 'gy'), 'gz'), may hold values from -3 to 3
- state_var: float32 [256, 256], P(('gx', 'gy'), 'gz'), may hold values from -1 to 1
- normal_a: float32 [256, 256], P(('gx', 'gy'), 'gz'), may hold values from 1 to 3
Outputs:
- displacement: float32 [256, 256, 256], P('gx', 'gy', 'gz')
- slip_rate: float32 [256, 256], P(('gx', 'gy'), 'gz')
All inputs are finite; a program needn't handle non-finite values.
Results may differ from a plain program's by a relative error of at most 0.0003.
Values sent between devices are 32-bit elements; how exact they have to be, the bound alone decides.
A program may use at most 128 MiB of HBM per device.

v0:
```python
import jax
import jax.numpy as jnp
from jax import lax
from jax.experimental import pallas as pl
from jax.experimental.pallas import tpu as pltpu
from jax.sharding import PartitionSpec as P

MESH = pl.DeviceIdType.MESH
AXES = ("gx", "gy", "gz")
PAD = 8
CHUNK = 8
GROUP = 2


def total(values):
    return jnp.sum(values.reshape(-1, 8, values.shape[-1]), axis=0)


def solve(t0, s):
    t1 = t0 - s[0]
    t2 = t1 - s[1]
    tiny = 1e-7
    p0 = s[0]
    l10 = s[1] / p0
    l20 = s[2] / p0
    p1 = s[2] - l10 * s[1]
    q = s[3] - l20 * s[1]
    ok1 = p1 > tiny * s[2]
    i1 = jnp.where(ok1, 1.0 / jnp.where(ok1, p1, 1.0), 0.0)
    l21 = q * i1
    p2 = s[4] - l20 * s[2] - l21 * q
    ok2 = ok1 & (p2 > tiny * s[4])
    i2 = jnp.where(ok2, 1.0 / jnp.where(ok2, p2, 1.0), 0.0)
    y1 = t1 - l10 * t0
    y2 = t2 - l20 * t0 - l21 * y1
    c2 = y2 * i2
    c1 = y1 * i1 - l21 * c2
    c0 = t0 / p0 - l10 * c1 - l20 * c2
    return c0, c1, c2


def parts_of(nx):
    inner = nx - 4
    runs = max(n for n in range(1, 7) if inner % (GROUP * n) == 0)
    size = inner // runs
    return [(0, 2), (nx - 2, 2)] + [(2 + n * size, size) for n in range(runs)]


def halves(values):
    high = values.astype(jnp.bfloat16)
    return high, (values - high.astype(jnp.float32)).astype(jnp.bfloat16)


def make_kernel(sizes):
    ngx, ngy, ngz = sizes
    count = ngx * ngy * ngz

    def kernel(load, stiff, pre_ref, state_ref, norm_ref, u0, u1, u2, coef_ref, slip,
               b, d, ysend, yrecv, zrecv, band, zterm, fsend, frecv, red,
               in_sem, send_sem, recv_sem, zs_sem, zr_sem, fs_sem, fr_sem, rs_sem, rr_sem):
        nx, ny, nz = b.shape
        us = (u0, u1, u2)
        ix, iy, iz = (lax.axis_index(a) for a in AXES)
        me = (ix * ngy + iy) * ngz + iz
        spots = (ix, iy, iz)

        def other(step):
            who = lax.rem(me + step, count)
            return (who // (ngy * ngz), lax.rem(who // ngz, ngy), lax.rem(who, ngz))

        parts = parts_of(nx)
        copies = []
        for n, (at, size) in enumerate(parts):
            part = pl.ds(at, size)
            copies.append((
                pltpu.make_async_copy(load.at[part], b.at[part], in_sem.at[0, n]),
                pltpu.make_async_copy(stiff.at[part], d.at[part], in_sem.at[1, n]),
            ))
            for one in copies[n]:
                one.start()

        barrier = pltpu.get_barrier_semaphore()

        @pl.loop(1, count)
        def _(step):
            pl.semaphore_signal(barrier, inc=1, device_id=other(step), device_id_type=MESH)

        zero_plane = jnp.zeros((2, ny, nz), jnp.float32)
        zero_rows = jnp.zeros((nx, 2, nz), jnp.float32)
        for k in range(3):
            @pl.when(ix == 0)
            def _():
                us[k][0:2, PAD:PAD + ny, :] = zero_plane
            @pl.when(ix == ngx - 1)
            def _():
                us[k][nx + 2:nx + 4, PAD:PAD + ny, :] = zero_plane
            @pl.when(iy == 0)
            def _():
                yrecv[k, 0] = zero_rows
            @pl.when(iy == ngy - 1)
            def _():
                yrecv[k, 1] = zero_rows

        row = lax.broadcasted_iota(jnp.int32, (nz, nz), 0)
        col = lax.broadcasted_iota(jnp.int32, (nz, nz), 1)
        far = row + jnp.where(iz == 0, nz, -nz)
        for n, at in enumerate((row, far, row, far)):
            gap = col - at
            full = jnp.where(jnp.abs(gap) == 1, 16.0, 0.0) - jnp.where(jnp.abs(gap) == 2, 1.0, 0.0)
            half = jnp.where(gap == 1, 16.0, 0.0) - jnp.where(gap == 2, 1.0, 0.0)
            band[0, n * nz:(n + 1) * nz, :] = full.astype(jnp.bfloat16)
            band[1, n * nz:(n + 1) * nz, :] = half.astype(jnp.bfloat16)

        def place(x, value, k):
            us[k][x + 2, PAD:PAD + ny, :] = value
            ysend[k, 0, x] = value[0:2]
            ysend[k, 1, x] = value[ny - 2:ny]

        def xcopy(k, side):
            u = us[k]
            if side == 0:
                src, dst, to = u.at[2:4, PAD:PAD + ny], u.at[nx + 2:nx + 4, PAD:PAD + ny], ix - 1
            else:
                src, dst, to = u.at[nx:nx + 2, PAD:PAD + ny], u.at[0:2, PAD:PAD + ny], ix + 1
            return pltpu.make_async_remote_copy(
                src, dst, send_sem.at[k, side], recv_sem.at[k, side],
                device_id=(to, iy, iz), device_id_type=MESH)

        def ycopy(k, side):
            to = iy - 1 if side == 0 else iy + 1
            return pltpu.make_async_remote_copy(
                ysend.at[k, side], yrecv.at[k, 1 - side], send_sem.at[k, 2 + side],
                recv_sem.at[k, 2 + side], device_id=(ix, to, iz), device_id_type=MESH)

        strips = ((8, ny - 8), (0, 8), (ny - 8, ny))

        def zcopy(k, at, size, n, strip):
            lo, hi = (0, ny) if strip is None else strips[strip]
            which = 0 if strip is None else strip
            return pltpu.make_async_remote_copy(
                us[k].at[pl.ds(at + 2, size), PAD + lo:PAD + hi], zrecv.at[k, pl.ds(at, size), lo:hi],
                zs_sem.at[k, n, which], zr_sem.at[k, n, which],
                device_id=(ix, iy, 1 - iz), device_id_type=MESH)

        def strips_of(n):
            return (None,) if n < 2 else (0, 1, 2)

        def sending(spot, size, side):
            return spot > 0 if side == 0 else spot < size - 1

        def receiving(spot, size, side):
            return spot < size - 1 if side == 0 else spot > 0

        def sides(k):
            return (1,) if k == 2 else (0, 1)

        def each(make, k, spot, size, test, act):
            for side in sides(k):
                @pl.when(test(spot, size, side))
                def _():
                    act(make(k, side))

        def start_x(k):
            each(xcopy, k, ix, ngx, sending, lambda c: c.start())

        def start_y(k):
            each(ycopy, k, iy, ngy, sending, lambda c: c.start())

        def scale(x, t0):
            inv = 1.0 / (7.5 + d[x])
            d[x] = inv
            rhs = b[x]
            value = inv * rhs
            place(x, value, 0)
            return t0 + total(value * rhs)

        t0 = jnp.zeros((8, nz), jnp.float32)
        for n, (at, size) in enumerate(parts):
            for one in copies[n]:
                one.wait()
            t0 = lax.fori_loop(at, at + size, scale, t0)
            if n == 1:
                pl.semaphore_wait(barrier, count - 1)
                start_x(0)
                zcopy(0, *parts[0], 0, None).start()
            if n >= 1:
                for strip in strips_of(n):
                    zcopy(0, at, size, n, strip).start()
        start_y(0)

        def wait_y(k):
            each(ycopy, k, iy, ngy, receiving, lambda c: c.wait_recv())

        def wait_x(k):
            each(xcopy, k, ix, ngx, receiving, lambda c: c.wait_recv())

        def along_z(k, at, size, lo, hi, which):
            rows = size * (hi - lo)
            own = us[k][pl.ds(at + 2, size), PAD + lo:PAD + hi, :].reshape(rows, nz)
            next_to = zrecv[k, pl.ds(at, size), lo:hi, :].reshape(rows, nz)
            own_high, own_low = halves(own)
            next_high, next_low = halves(next_to)
            lhs = jnp.concatenate([own_high, next_high, own_low, next_low], axis=1)
            found = jnp.dot(lhs, band[which], preferred_element_type=jnp.float32)
            zterm[pl.ds(at, size), lo:hi, :] = found.reshape(size, hi - lo, nz)

        def near(k, x, lo, hi):
            u = us[k]
            lo, hi = lo + PAD, hi + PAD
            one = (u[x + 1, lo:hi, :] + u[x + 3, lo:hi, :]
                   + u[x + 2, lo - 1:hi - 1, :] + u[x + 2, lo + 1:hi + 1, :])
            two = (u[x, lo:hi, :] + u[x + 4, lo:hi, :]
                   + u[x + 2, lo - 2:hi - 2, :] + u[x + 2, lo + 2:hi + 2, :])
            return (16.0 * one - two + zterm[x, lo - PAD:hi - PAD, :]) * (1.0 / 12.0)

        def half_near(k, x, lo, hi):
            u = us[k]
            lo, hi = lo + PAD, hi + PAD
            one = u[x + 1, lo:hi, :] + u[x + 2, lo - 1:hi - 1, :]
            two = u[x, lo:hi, :] + u[x + 2, lo - 2:hi - 2, :]
            return (16.0 * one - two + zterm[x, lo - PAD:hi - PAD, :]) * (1.0 / 6.0)

        zero = jnp.zeros((8, nz), jnp.float32)

        def run(block, k, carry, which, finish):
            first_at, size = parts[2]

            def part(n, carry):
                at = first_at + n * size
                zcopy(k, at, size, n + 2, 0).wait_recv()
                along_z(k, at, size, *strips[0], which)

                def inner(i, carry):
                    for g in range(GROUP):
                        carry = block(at + i * GROUP + g, *strips[0], carry)
                    return carry

                carry = lax.fori_loop(0, size // GROUP, inner, carry)
                if k < 2:
                    zcopy(k + 1, at, size, n + 2, 0).start()
                return carry

            carry = lax.fori_loop(0, len(parts) - 2, part, carry)
            for n, (at, size) in enumerate(parts):
                for strip in strips_of(n):
                    if strip != 0:
                        zcopy(k, at, size, n, strip).wait_recv()
                if n < 2:
                    along_z(k, at, size, 0, ny, which)
            for strip in (1, 2):
                along_z(k, 2, nx - 4, *strips[strip], which)
            wait_y(k)

            def rim(i, carry):
                for g in range(GROUP):
                    x = i * GROUP + g
                    us[k][x + 2, PAD - 2:PAD, :] = yrecv[k, 0, x]
                    us[k][x + 2, PAD + ny:PAD + ny + 2, :] = yrecv[k, 1, x]
                    carry = block(x, 0, 8, carry)
                    carry = block(x, ny - 8, ny, carry)
                return carry

            def whole(n, carry):
                x = jnp.where(n < 2, n, nx - 4 + n)
                us[k][x + 2, PAD - 2:PAD, :] = yrecv[k, 0, x]
                us[k][x + 2, PAD + ny:PAD + ny + 2, :] = yrecv[k, 1, x]
                carry = block(x, 0, ny, carry)
                return carry

            carry = lax.fori_loop(1, nx // GROUP - 1, rim, carry)
            wait_x(k)
            carry = lax.fori_loop(0, 4, whole, carry)
            finish()
            return carry

        def advance(k):
            def block(x, lo, hi, carry):
                even, odd = carry
                value = us[k][x + 2, PAD + lo:PAD + hi, :]
                w = near(k, x, lo, hi)
                fresh = d[x, lo:hi, :] * w
                even = even + total(value * (b[x, lo:hi, :] - w))
                odd = odd + total((value - fresh) * w)
                b[x, lo:hi, :] = w
                us[k + 1][x + 2, PAD + lo:PAD + hi, :] = fresh
                if lo == 0:
                    ysend[k + 1, 0, x] = fresh[0:2]
                if hi == ny:
                    ysend[k + 1, 1, x] = fresh[hi - lo - 2:hi - lo]
                return even, odd

            def finish():
                start_x(k + 1)
                start_y(k + 1)
                for n, (at, size) in enumerate(parts):
                    for strip in strips_of(n):
                        if strip != 0:
                            zcopy(k + 1, at, size, n, strip).start()

            return run(block, k, (zero, zero), 0, finish)

        s0, s1 = advance(0)
        s2, s3 = advance(1)

        owned = nx // ngy
        below = iy == ngy // 2 - 1
        above = iy == ngy // 2

        def fault_copy(which, to):
            return pltpu.make_async_remote_copy(
                fsend.at[:, pl.ds(to * owned, owned), :], frecv.at[which], fs_sem.at[to], fr_sem.at[which],
                device_id=(ix, to, iz), device_id_type=MESH)

        @pl.when(below | above)
        def _():
            edge = jnp.where(below, 1, 0)
            front = jnp.where(below, 1.0 / 24.0, 27.0 / 24.0)
            close = jnp.where(below, -27.0 / 24.0, -1.0 / 24.0)

            @pl.loop(0, nx)
            def _(x):
                for j in range(3):
                    rows = ysend[j, edge, x]
                    fsend[j, pl.ds(x, 1), :] = front * rows[0:1] + close * rows[1:2]

        for which, owner in enumerate((ngy // 2 - 1, ngy // 2)):
            @pl.when(iy == owner)
            def _():
                for to in range(ngy):
                    if to != owner:
                        fault_copy(which, to).start()
                frecv[which] = fsend[:, owner * owned:(owner + 1) * owned, :]

        def last(x, lo, hi, s4):
            value = us[2][x + 2, PAD + lo:PAD + hi, :]
            return s4 + total(value * (b[x, lo:hi, :] - half_near(2, x, lo, hi)))

        s4 = run(last, 2, zero, 1, lambda: None)

        slot = lax.broadcasted_iota(jnp.int32, (1, nz), 1)
        sent = jnp.zeros((1, nz), jnp.float32)
        for j, part in enumerate((t0, s0, s1, s2, s3, s4)):
            whole = jnp.sum(jnp.sum(part, axis=1, keepdims=True), axis=0, keepdims=True)
            sent = sent + jnp.where(slot == j, whole, 0.0)
        red[me] = sent

        def sum_copy(step):
            return pltpu.make_async_remote_copy(
                red.at[me], red.at[me], rs_sem.at[step], rr_sem.at[me],
                device_id=other(step), device_id_type=MESH)

        @pl.loop(1, count)
        def _(step):
            sum_copy(step).start()

        @pl.loop(1, count)
        def _(step):
            who = lax.rem(me + step, count)
            pltpu.make_async_remote_copy(
                red.at[who], red.at[who], rs_sem.at[step], rr_sem.at[who],
                device_id=other(step), device_id_type=MESH).wait_recv()

        sums = jnp.sum(red[...], axis=0)
        sums = [jnp.sum(jnp.where(slot == j, sums, 0.0), axis=1, keepdims=True) for j in range(6)]
        coefs = [jnp.broadcast_to(c, (1, nz)) for c in solve(sums[0], sums[1:])]

        for j in range(3):
            coef_ref[j:j + 1, :] = coefs[j]

        for which, owner in enumerate((ngy // 2 - 1, ngy // 2)):
            @pl.when(iy != owner)
            def _():
                fault_copy(which, owner).wait_recv()
        traction = sum(coefs[j] * (frecv[0, j] + frecv[1, j]) for j in range(3))
        arg = (pre_ref[...] + 2.0 * traction) / norm_ref[...]
        half = jnp.float32(-0.6931471805599453)
        small = arg * (1.0 + arg * arg * (1.0 / 6.0) * (1.0 + arg * arg * 0.05))
        sinh = jnp.where(jnp.abs(arg) < 0.25, small, jnp.exp(arg + half) - jnp.exp(half - arg))
        slip[...] = jnp.exp(-state_ref[...]) * sinh

        for k in range(3):
            each(xcopy, k, ix, ngx, sending, lambda c: c.wait_send())
            each(ycopy, k, iy, ngy, sending, lambda c: c.wait_send())
            for n, (at, size) in enumerate(parts):
                for strip in strips_of(n):
                    zcopy(k, at, size, n, strip).wait_send()
        for which, owner in enumerate((ngy // 2 - 1, ngy // 2)):
            @pl.when(iy == owner)
            def _():
                for to in range(ngy):
                    if to != owner:
                        fault_copy(which, to).wait_send()

        @pl.loop(1, count)
        def _(step):
            sum_copy(step).wait_send()

    return kernel


def blend(u0, u1, u2, coef_ref, out, obuf, out_sem):
    nx, ny, nz = obuf.shape
    mid = slice(PAD, PAD + ny)
    coefs = [coef_ref[j:j + 1, :] for j in range(3)]

    def out_copy(c):
        part = pl.ds(c * CHUNK, CHUNK)
        return pltpu.make_async_copy(obuf.at[part], out.at[part], out_sem.at[c])

    def plane(x, carry):
        obuf[x] = (coefs[0] * u0[x + 2, mid, :] + coefs[1] * u1[x + 2, mid, :]
                   + coefs[2] * u2[x + 2, mid, :])
        return carry

    for c in range(nx // CHUNK):
        lax.fori_loop(c * CHUNK, (c + 1) * CHUNK, plane, 0)
        out_copy(c).start()
    for c in range(nx // CHUNK):
        out_copy(c).wait()


def solution(mesh):
    sizes = tuple(mesh.shape[a] for a in AXES)
    assert sizes[1] % 2 == 0 and sizes[2] == 2

    def per_device(load, stiffness, prestress, state_var, normal_a):
        nx, ny, nz = load.shape
        assert nx % CHUNK == 0
        runs = len(parts_of(nx))
        f32 = jnp.float32
        count = sizes[0] * sizes[1] * sizes[2]
        padded = (nx + 4, ny + 2 * PAD, nz)
        vmem = pl.BlockSpec(memory_space=pltpu.VMEM)
        hbm = pl.BlockSpec(memory_space=pltpu.HBM)
        dma = pltpu.SemaphoreType.DMA
        u0, u1, u2, coefs, slip = pl.pallas_call(
            make_kernel(sizes),
            out_shape=(
                pltpu.VMEM(padded, f32),
                pltpu.VMEM(padded, f32),
                pltpu.VMEM(padded, f32),
                pltpu.VMEM((8, nz), f32),
                jax.ShapeDtypeStruct(prestress.shape, f32),
            ),
            in_specs=[hbm, hbm, vmem, vmem, vmem],
            out_specs=(vmem,) * 5,
            scratch_shapes=[
                pltpu.VMEM((nx, ny, nz), f32),
                pltpu.VMEM((nx, ny, nz), f32),
                pltpu.VMEM((3, 2, nx, 2, nz), f32),
                pltpu.VMEM((3, 2, nx, 2, nz), f32),
                pltpu.VMEM((3, nx, ny, nz), f32),
                pltpu.VMEM((2, 4 * nz, nz), jnp.bfloat16),
                pltpu.VMEM((nx, ny, nz), f32),
                pltpu.VMEM((3, nx, nz), f32),
                pltpu.VMEM((2, 3, nx // sizes[1], nz), f32),
                pltpu.VMEM((count, 1, nz), f32),
                dma((2, runs)),
                dma((3, 4)),
                dma((3, 4)),
                dma((3, runs, 3)),
                dma((3, runs, 3)),
                dma((sizes[1],)),
                dma((2,)),
                dma((count,)),
                dma((count,)),
            ],
            compiler_params=pltpu.CompilerParams(
                collective_id=0, has_side_effects=True, vmem_limit_bytes=54 * 2**20),
        )(load, stiffness, prestress, state_var, normal_a)
        displacement = pl.pallas_call(
            blend,
            out_shape=jax.ShapeDtypeStruct(load.shape, f32),
            in_specs=[vmem] * 4,
            out_specs=hbm,
            scratch_shapes=[pltpu.VMEM((nx, ny, nz), f32), dma((nx // CHUNK,))],
            compiler_params=pltpu.CompilerParams(vmem_limit_bytes=8 * 2**20),
        )(u0, u1, u2, coefs)
        return displacement, slip

    placed = (
        P("gx", "gy", "gz"),
        P("gx", "gy", "gz"),
        P(("gx", "gy"), "gz"),
        P(("gx", "gy"), "gz"),
        P(("gx", "gy"), "gz"),
    )
    return jax.shard_map(
        per_device,
        mesh=mesh,
        in_specs=placed,
        out_specs=(P("gx", "gy", "gz"), P(("gx", "gy"), "gz")),
        check_vma=False,
    )
```

profile of v0, /device:TPU:0, one launch (start us, length us, event | category | flops | bytes accessed | tf_op | source)
XLA Modules:
  0.0 33.3 jit_solution(2097898246388389012)
XLA Ops:
  0.6 30.5 %shard_map.68 = (f32[68,80,128]{2,1,0:T(8,128)S(1)}, f32[68,80,128]{2,1,0:T(8,128)S(1)}, f32[68,80,128]{2,1,0:T(8,128)S(1)}, f32[8,128]{1,0:T(8,128)S(1)}, f32[16,128]{1,0:T(8,128)}) custom-call(f32[64,64,128]{2,1,0:T(8,128)} %load.1, f32[64,64,128]{2,1,0:T(8,128)} %stiff.1, f32[16,128]{1,0:T(8,128)} %pre_ref.1, f32[16,128]{1,0:T(8,128)} %state_ref.1, ...), custom_call_target="tpu_custom_call" | custom-call | tf_op jit(solution)/shard_map/pallas_call | solution.py:436
  31.1 0.0 copy-start
  31.2 1.5 %shard_map.69 = f32[64,64,128]{2,1,0:T(8,128)} custom-call(f32[68,80,128]{2,1,0:T(8,128)S(1)} %get-tuple-element.7.u0, f32[68,80,128]{2,1,0:T(8,128)S(1)} %get-tuple-element.8.u1, f32[68,80,128]{2,1,0:T(8,128)S(1)} %get-tuple-element.9.u2, f32[8,128]{1,0:T(8,128)S(1)} %get-tuple-element.10.coef_ref), custom_call_target="tpu_custom_call" | custom-call | tf_op jit(solution)/shard_map/pallas_call | solution.py:471
  32.6 0.0 copy-done
  32.7 0.6 %copy.8 = f32[16,128]{1,0:T(8,128)} copy(f32[16,128]{1,0:T(8,128)S(1)} %copy-done) | data formatting | bytes 16384
Async XLA Ops:
  31.1 1.5 %copy-start = (f32[16,128]{1,0:T(8,128)S(1)}, f32[16,128]{1,0:T(8,128)}, u32[]{:S(2)}) copy-start(f32[16,128]{1,0:T(8,128)} %get-tuple-element.15) | copy-start | bytes 24580
where the time goes:
time: 33.5 us; the launch traced here: 33.3 us
  Pallas kernels  32 us (96%)
  between operations  0.66 us (2%)
  local copies, waits for them, and re-layouts  0.61 us (2%)
    pallas_call x1, Pallas kernels, per_device(): pl.pallas_call(make_kernel(sizes), out_shape=(pltpu.VMEM(padded, f32), pl...  30.5 us
    pallas_call x1, Pallas kernels, per_device(): pl.pallas_call(blend, out_shape=jax.ShapeDtypeStruct(load.shape, f32), in...  1.49 us

commit v1 on v0

--- a/solution.py
+++ b/solution.py
@@ -55,18 +55,20 @@
     ngx, ngy, ngz = sizes
     count = ngx * ngy * ngz
 
-    def kernel(load, stiff, pre_ref, state_ref, norm_ref, u0, u1, u2, coef_ref, slip,
-               b, d, ysend, yrecv, zrecv, band, zterm, fsend, frecv, red,
-               in_sem, send_sem, recv_sem, zs_sem, zr_sem, fs_sem, fr_sem, rs_sem, rr_sem):
+    def kernel(load, stiff, u0, u1, u2, coef_ref, frecv,
+               b, d, ysend, yrecv, zrecv, band, zterm, fsend, red,
+               in_sem, send_sem, recv_sem, zs_sem, zr_sem, fs_sem, fr_sem, rs_sem, rr_sem,
+               row_sem, all_sem):
         nx, ny, nz = b.shape
         us = (u0, u1, u2)
         ix, iy, iz = (lax.axis_index(a) for a in AXES)
         me = (ix * ngy + iy) * ngz + iz
-        spots = (ix, iy, iz)
-
-        def other(step):
-            who = lax.rem(me + step, count)
-            return (who // (ngy * ngz), lax.rem(who // ngz, ngy), lax.rem(who, ngz))
+
+        def around(spot, size):
+            moved = [spot + n for n in range(size)]
+            return [spot] + [jnp.where(m >= size, m - size, m) for m in moved[1:]]
+
+        xs, ys, zs = around(ix, ngx), around(iy, ngy), around(iz, ngz)
 
         parts = parts_of(nx)
         copies = []
@@ -81,9 +83,10 @@
 
         barrier = pltpu.get_barrier_semaphore()
 
-        @pl.loop(1, count)
-        def _(step):
-            pl.semaphore_signal(barrier, inc=1, device_id=other(step), device_id_type=MESH)
+        in_line = ([(ix, iy, z) for z in zs[1:]] + [(x, iy, iz) for x in xs[1:]]
+                   + [(ix, y, iz) for y in ys[1:]])
+        for who in in_line:
+            pl.semaphore_signal(barrier, inc=1, device_id=who, device_id_type=MESH)
 
         zero_plane = jnp.zeros((2, ny, nz), jnp.float32)
         zero_rows = jnp.zeros((nx, 2, nz), jnp.float32)
@@ -180,7 +183,9 @@
                 one.wait()
             t0 = lax.fori_loop(at, at + size, scale, t0)
             if n == 1:
-                pl.semaphore_wait(barrier, count - 1)
+                pl.semaphore_wait(barrier, len(in_line))
+                for y in ys[1:]:
+                    pl.semaphore_signal(row_sem, inc=1, device_id=(ix, y, iz), device_id_type=MESH)
                 start_x(0)
                 zcopy(0, *parts[0], 0, None).start()
             if n >= 1:
@@ -300,6 +305,9 @@
             return run(block, k, (zero, zero), 0, finish)
 
         s0, s1 = advance(0)
+        pl.semaphore_wait(row_sem, ngy - 1)
+        for z in zs[1:]:
+            pl.semaphore_signal(all_sem, inc=1, device_id=(ix, iy, z), device_id_type=MESH)
         s2, s3 = advance(1)
 
         owned = nx // ngy
@@ -335,49 +343,32 @@
             value = us[2][x + 2, PAD + lo:PAD + hi, :]
             return s4 + total(value * (b[x, lo:hi, :] - half_near(2, x, lo, hi)))
 
+        slot = lax.broadcasted_iota(jnp.int32, (1, nz), 1)
+
+        def spread(parts):
+            sent = jnp.zeros((1, nz), jnp.float32)
+            for j, part in parts:
+                whole = jnp.sum(jnp.sum(part, axis=0, keepdims=True), axis=1, keepdims=True)
+                sent = sent + jnp.where(slot == j, whole, 0.0)
+            return sent
+
+        early = spread(list(enumerate((t0, s0, s1, s2, s3))))
         s4 = run(last, 2, zero, 1, lambda: None)
-
-        slot = lax.broadcasted_iota(jnp.int32, (1, nz), 1)
-        sent = jnp.zeros((1, nz), jnp.float32)
-        for j, part in enumerate((t0, s0, s1, s2, s3, s4)):
-            whole = jnp.sum(jnp.sum(part, axis=1, keepdims=True), axis=0, keepdims=True)
-            sent = sent + jnp.where(slot == j, whole, 0.0)
-        red[me] = sent
-
-        def sum_copy(step):
+        red[me] = early + spread([(5, s4)])
+        pl.semaphore_wait(all_sem, ngz - 1)
+
+        def sum_copy(who):
             return pltpu.make_async_remote_copy(
-                red.at[me], red.at[me], rs_sem.at[step], rr_sem.at[me],
-                device_id=other(step), device_id_type=MESH)
-
-        @pl.loop(1, count)
-        def _(step):
-            sum_copy(step).start()
-
-        @pl.loop(1, count)
-        def _(step):
-            who = lax.rem(me + step, count)
-            pltpu.make_async_remote_copy(
-                red.at[who], red.at[who], rs_sem.at[step], rr_sem.at[who],
-                device_id=other(step), device_id_type=MESH).wait_recv()
-
-        sums = jnp.sum(red[...], axis=0)
-        sums = [jnp.sum(jnp.where(slot == j, sums, 0.0), axis=1, keepdims=True) for j in range(6)]
-        coefs = [jnp.broadcast_to(c, (1, nz)) for c in solve(sums[0], sums[1:])]
-
-        for j in range(3):
-            coef_ref[j:j + 1, :] = coefs[j]
+                red.at[me], red.at[me], rs_sem, rr_sem, device_id=who, device_id_type=MESH)
+
+        others = [(x, y, z) for y in reversed(ys) for x in reversed(xs) for z in reversed(zs)][:-1]
+        for who in others:
+            sum_copy(who).start()
 
         for which, owner in enumerate((ngy // 2 - 1, ngy // 2)):
             @pl.when(iy != owner)
             def _():
                 fault_copy(which, owner).wait_recv()
-        traction = sum(coefs[j] * (frecv[0, j] + frecv[1, j]) for j in range(3))
-        arg = (pre_ref[...] + 2.0 * traction) / norm_ref[...]
-        half = jnp.float32(-0.6931471805599453)
-        small = arg * (1.0 + arg * arg * (1.0 / 6.0) * (1.0 + arg * arg * 0.05))
-        sinh = jnp.where(jnp.abs(arg) < 0.25, small, jnp.exp(arg + half) - jnp.exp(half - arg))
-        slip[...] = jnp.exp(-state_ref[...]) * sinh
-
         for k in range(3):
             each(xcopy, k, ix, ngx, sending, lambda c: c.wait_send())
             each(ycopy, k, iy, ngy, sending, lambda c: c.wait_send())
@@ -391,14 +382,21 @@
                     if to != owner:
                         fault_copy(which, to).wait_send()
 
-        @pl.loop(1, count)
-        def _(step):
-            sum_copy(step).wait_send()
+        arrived = red.at[pl.ds(0, count - 1)]
+        everyone = pltpu.make_async_remote_copy(
+            arrived, arrived, rs_sem, rr_sem, device_id=others[0], device_id_type=MESH)
+        everyone.wait_recv()
+        sums = jnp.sum(red[...], axis=0)
+        sums = [jnp.sum(jnp.where(slot == j, sums, 0.0), axis=1, keepdims=True) for j in range(6)]
+        coefs = solve(sums[0], sums[1:])
+        for j in range(3):
+            coef_ref[j:j + 1, :] = jnp.broadcast_to(coefs[j], (1, nz))
+        everyone.wait_send()
 
     return kernel
 
 
-def blend(u0, u1, u2, coef_ref, out, obuf, out_sem):
+def blend(u0, u1, u2, coef_ref, fault, pre_ref, state_ref, norm_ref, out, slip, obuf, out_sem):
     nx, ny, nz = obuf.shape
     mid = slice(PAD, PAD + ny)
     coefs = [coef_ref[j:j + 1, :] for j in range(3)]
@@ -415,6 +413,12 @@
     for c in range(nx // CHUNK):
         lax.fori_loop(c * CHUNK, (c + 1) * CHUNK, plane, 0)
         out_copy(c).start()
+    traction = sum(coefs[j] * (fault[0, j] + fault[1, j]) for j in range(3))
+    arg = (pre_ref[...] + 2.0 * traction) / norm_ref[...]
+    half = jnp.float32(-0.6931471805599453)
+    small = arg * (1.0 + arg * arg * (1.0 / 6.0) * (1.0 + arg * arg * 0.05))
+    sinh = jnp.where(jnp.abs(arg) < 0.25, small, jnp.exp(arg + half) - jnp.exp(half - arg))
+    slip[...] = jnp.exp(-state_ref[...]) * sinh
     for c in range(nx // CHUNK):
         out_copy(c).wait()
 
@@ -433,16 +437,16 @@
         vmem = pl.BlockSpec(memory_space=pltpu.VMEM)
         hbm = pl.BlockSpec(memory_space=pltpu.HBM)
         dma = pltpu.SemaphoreType.DMA
-        u0, u1, u2, coefs, slip = pl.pallas_call(
+        u0, u1, u2, coefs, fault = pl.pallas_call(
             make_kernel(sizes),
             out_shape=(
                 pltpu.VMEM(padded, f32),
                 pltpu.VMEM(padded, f32),
                 pltpu.VMEM(padded, f32),
                 pltpu.VMEM((8, nz), f32),
-                jax.ShapeDtypeStruct(prestress.shape, f32),
+                pltpu.VMEM((2, 3, nx // sizes[1], nz), f32),
             ),
-            in_specs=[hbm, hbm, vmem, vmem, vmem],
+            in_specs=[hbm, hbm],
             out_specs=(vmem,) * 5,
             scratch_shapes=[
                 pltpu.VMEM((nx, ny, nz), f32),
@@ -453,7 +457,6 @@
                 pltpu.VMEM((2, 4 * nz, nz), jnp.bfloat16),
                 pltpu.VMEM((nx, ny, nz), f32),
                 pltpu.VMEM((3, nx, nz), f32),
-                pltpu.VMEM((2, 3, nx // sizes[1], nz), f32),
                 pltpu.VMEM((count, 1, nz), f32),
                 dma((2, runs)),
                 dma((3, 4)),
@@ -462,20 +465,25 @@
                 dma((3, runs, 3)),
                 dma((sizes[1],)),
                 dma((2,)),
-                dma((count,)),
-                dma((count,)),
+                dma,
+                dma,
+                pltpu.SemaphoreType.REGULAR,
+                pltpu.SemaphoreType.REGULAR,
             ],
             compiler_params=pltpu.CompilerParams(
                 collective_id=0, has_side_effects=True, vmem_limit_bytes=54 * 2**20),
-        )(load, stiffness, prestress, state_var, normal_a)
-        displacement = pl.pallas_call(
+        )(load, stiffness)
+        displacement, slip = pl.pallas_call(
             blend,
-            out_shape=jax.ShapeDtypeStruct(load.shape, f32),
-            in_specs=[vmem] * 4,
-            out_specs=hbm,
+            out_shape=(
+                jax.ShapeDtypeStruct(load.shape, f32),
+                jax.ShapeDtypeStruct(prestress.shape, f32),
+            ),
+            in_specs=[vmem] * 8,
+            out_specs=(hbm, vmem),
             scratch_shapes=[pltpu.VMEM((nx, ny, nz), f32), dma((nx // CHUNK,))],
             compiler_params=pltpu.CompilerParams(vmem_limit_bytes=8 * 2**20),
-        )(u0, u1, u2, coefs)
+        )(u0, u1, u2, coefs, fault, prestress, state_var, normal_a)
         return displacement, slip
 
     placed = (

time: 33.5 us -> 30.2 us (0.901)
  Pallas kernels: 32 us -> 29.3 us
  local copies, waits for them, and re-layouts: 0.61 us -> 0.01 us
    pallas_call x1, Pallas kernels: 30.5 us -> 27.2 us  [per_device(): pl.pallas_call(make_kernel(sizes), out_shape=(pltpu.VMEM(padded, f32), pl...]
    pallas_call x1, Pallas kernels: 1.49 us -> 2.08 us  [per_device(): pl.pallas_call(blend, out_shape=(jax.ShapeDtypeStruct(load.shape, f32), j...]
    unnamed x3 -> x6, local copies, waits for them, and re-layouts: 0.61 us -> 0.01 us
where the time goes in v1:
time: 30.2 us; the launch traced here: 30 us
  Pallas kernels  29.3 us (97%)
  between operations  0.69 us (2%)
    pallas_call x1, Pallas kernels, per_device(): pl.pallas_call(make_kernel(sizes), out_shape=(pltpu.VMEM(padded, f32), pl...  27.2 us
    pallas_call x1, Pallas kernels, per_device(): pl.pallas_call(blend, out_shape=(jax.ShapeDtypeStruct(load.shape, f32), j...  2.08 us

profile of v1, /device:TPU:0, one launch (start us, length us, event | category | flops | bytes accessed | tf_op | source)
XLA Modules:
  0.0 30.0 jit_solution(1022509966567153891)
XLA Ops:
  0.6 0.0 copy-start.2
  0.6 0.0 copy-start.1
  0.7 0.0 copy-start
  0.7 27.2 %shard_map.68 = (f32[68,80,128]{2,1,0:T(8,128)S(1)}, f32[68,80,128]{2,1,0:T(8,128)S(1)}, f32[68,80,128]{2,1,0:T(8,128)S(1)}, f32[8,128]{1,0:T(8,128)S(1)}, f32[2,3,16,128]{3,2,1,0:T(8,128)S(1)}) custom-call(f32[64,64,128]{2,1,0:T(8,128)} %load.1, f32[64,64,128]{2,1,0:T(8,128)} %stiff.1), custom_call_target="tpu_custom_call" | custom-call | tf_op jit(solution)/shard_map/pallas_call | solution.py:440
  27.9 0.0 copy-done.2
  27.9 0.0 copy-done.1
  27.9 0.0 copy-done
  27.9 2.1 %shard_map.69 = (f32[64,64,128]{2,1,0:T(8,128)}, f32[16,128]{1,0:T(8,128)}) custom-call(f32[68,80,128]{2,1,0:T(8,128)S(1)} %get-tuple-element.7.u0, f32[68,80,128]{2,1,0:T(8,128)S(1)} %get-tuple-element.8.u1, f32[68,80,128]{2,1,0:T(8,128)S(1)} %get-tuple-element.9.u2, f32[8,128]{1,0:T(8,128)S(1)} %get-tuple-element.10.coef_ref, ...), custom_call_target="tpu_custom_call" | custom-call | tf_op jit(solution)/shard_map/pallas_call | solution.py:476
Async XLA Ops:
  0.6 27.3 %copy-start.2 = (f32[16,128]{1,0:T(8,128)S(1)}, f32[16,128]{1,0:T(8,128)}, u32[]{:S(2)}) copy-start(f32[16,128]{1,0:T(8,128)} %norm_ref.1) | copy-start | bytes 24580
  0.6 27.3 %copy-start.1 = (f32[16,128]{1,0:T(8,128)S(1)}, f32[16,128]{1,0:T(8,128)}, u32[]{:S(2)}) copy-start(f32[16,128]{1,0:T(8,128)} %state_ref.1) | copy-start | bytes 24580
  0.7 27.3 %copy-start = (f32[16,128]{1,0:T(8,128)S(1)}, f32[16,128]{1,0:T(8,128)}, u32[]{:S(2)}) copy-start(f32[16,128]{1,0:T(8,128)} %pre_ref.1) | copy-start | bytes 24580

commit v2 on v1

v2 whole, which is shorter than its diff:
```python
import functools
import itertools
import jax
import jax.numpy as jnp
from jax import lax
from jax.experimental import pallas as pl
from jax.experimental.pallas import tpu as pltpu
from jax.sharding import PartitionSpec as P

MESH = pl.DeviceIdType.MESH
AXES = ("gx", "gy", "gz")
PAD = 8
CHUNK = 8
LOADS = 2


def total(values):
    return jnp.sum(values.reshape(-1, 8, values.shape[-1]), axis=0)


def solve(t0, s):
    t1 = t0 - s[0]
    t2 = t1 - s[1]
    tiny = 1e-7
    p0 = s[0]
    l10 = s[1] / p0
    l20 = s[2] / p0
    p1 = s[2] - l10 * s[1]
    q = s[3] - l20 * s[1]
    ok1 = p1 > tiny * s[2]
    i1 = jnp.where(ok1, 1.0 / jnp.where(ok1, p1, 1.0), 0.0)
    l21 = q * i1
    p2 = s[4] - l20 * s[2] - l21 * q
    ok2 = ok1 & (p2 > tiny * s[4])
    i2 = jnp.where(ok2, 1.0 / jnp.where(ok2, p2, 1.0), 0.0)
    y1 = t1 - l10 * t0
    y2 = t2 - l20 * t0 - l21 * y1
    c2 = y2 * i2
    c1 = y1 * i1 - l21 * c2
    c0 = t0 / p0 - l10 * c1 - l20 * c2
    return c0, c1, c2


def divisor(n, most):
    return max(m for m in range(1, most + 1) if n % m == 0)


def halves(values):
    high = values.astype(jnp.bfloat16)
    return high, (values - high.astype(jnp.float32)).astype(jnp.bfloat16)


def radii(sizes):
    needed = sum(n - 1 for n in sizes)
    hops, reached = [], 1
    while reached < needed or len(hops) < 2:
        hops.append(min(reached, max(needed - reached, 1)))
        reached += hops[-1]
    return hops


def make_kernel(sizes):
    ngx, ngy, ngz = sizes
    count = ngx * ngy * ngz

    def kernel(load, stiff, u0, u1, u2, coef_ref, frecv,
               b, d, ysend, yrecv, zsend, zrecv, rsend, rrecv, band, zterm, fsend, red,
               in_sem, send_sem, recv_sem, zs_sem, zr_sem, fs_sem, fr_sem, rs_sem, rr_sem,
               known):
        nx, ny, nz = b.shape
        us = (u0, u1, u2)
        ix, iy, iz = (lax.axis_index(a) for a in AXES)
        me = (ix * ngy + iy) * ngz + iz
        half = (nx - 4) // 2
        size = divisor(half, 10)
        window = divisor(size, 5)
        piece = half // LOADS
        strip = divisor(nx - 4, 6)
        border_run = divisor(nx - 4, 30)
        mid = tuple(range(8, ny - 8, 8))
        ends = (0, ny - 8)
        full = tuple(range(0, ny, 8))

        def around(spot, size):
            moved = [spot + n for n in range(size)]
            return [spot] + [jnp.where(m >= size, m - size, m) for m in moved[1:]]

        xs, ys, zs = around(ix, ngx), around(iy, ngy), around(iz, ngz)

        sources = ((load, b), (stiff, d))
        for src, dst in sources:
            for at in (0, nx - 2):
                pltpu.make_async_copy(src.at[at:at + 2], dst.at[at:at + 2], in_sem.at[0]).start()
        for src, dst in sources:
            for at in ends:
                pltpu.make_async_copy(
                    src.at[2:nx - 2, at:at + 8], dst.at[2:nx - 2, at:at + 8], in_sem.at[1]).start()
        for n in range(2 * LOADS):
            part = pl.ds(2 + n * piece, piece)
            for src, dst in sources:
                pltpu.make_async_copy(
                    src.at[part, 8:ny - 8], dst.at[part, 8:ny - 8], in_sem.at[2 + n]).start()

        def loaded(ref, n):
            pltpu.make_async_copy(ref, ref, in_sem.at[n]).wait()

        barrier = pltpu.get_barrier_semaphore()
        spots = (ix, iy, iz)

        def ball(radius):
            reach = [range(-min(radius, n - 1), min(radius, n - 1) + 1) for n in sizes]
            for step in itertools.product(*reach):
                if 0 < sum(abs(g) for g in step) <= radius:
                    inside = [spot + g >= 0 if g < 0 else spot + g < n
                              for spot, g, n in zip(spots, step, sizes) if g]
                    yield functools.reduce(jnp.logical_and, inside), tuple(
                        spot + g for spot, g in zip(spots, step))

        def tell(sem, radius):
            for there, who in ball(radius):
                @pl.when(there)
                def _():
                    pl.semaphore_signal(sem, inc=1, device_id=who, device_id_type=MESH)

        def hear(sem, radius):
            pl.semaphore_wait(sem, sum(jnp.where(there, 1, 0) for there, _ in ball(radius)))

        hops = radii(sizes)
        tell(barrier, 1)

        zero_plane = jnp.zeros((2, ny, nz), jnp.float32)
        zero_rows = jnp.zeros((nx, 2, nz), jnp.float32)
        for k in range(3):
            @pl.when(ix == 0)
            def _():
                us[k][0:2, PAD:PAD + ny, :] = zero_plane
            @pl.when(ix == ngx - 1)
            def _():
                us[k][nx + 2:nx + 4, PAD:PAD + ny, :] = zero_plane
            @pl.when(iy == 0)
            def _():
                yrecv[k, 0] = zero_rows
            @pl.when(iy == ngy - 1)
            def _():
                yrecv[k, 1] = zero_rows

        row = lax.broadcasted_iota(jnp.int32, (nz, nz), 0)
        col = lax.broadcasted_iota(jnp.int32, (nz, nz), 1)
        far = jnp.bitwise_and(col, 1) + jnp.where(iz == 0, nz, -2)

        def weights(gap, near):
            return jnp.where(near(gap) == 1, 16.0, 0.0) - jnp.where(near(gap) == 2, 1.0, 0.0)

        own = weights(col - row, jnp.abs)
        up = weights(col - row, lambda g: g)
        out = weights(far - row, jnp.abs).astype(jnp.bfloat16)
        for which, part in enumerate((own, up)):
            for n in range(2):
                band[which, n * nz:(n + 1) * nz, 0:nz] = part.astype(jnp.bfloat16)
                band[which, n * nz:(n + 1) * nz, nz:2 * nz] = out

        lane = lax.broadcasted_iota(jnp.int32, (8, nz), 1)
        pair = lane // 2
        edge_low = jnp.where(iz == 0, nz - 2, 0)
        at_edge = (lane >= edge_low) & (lane < edge_low + 2)
        at_upper = at_edge & (iz == 1)

        def xcopy(k, side):
            u = us[k]
            if side == 0:
                src, dst, to = u.at[2:4, PAD:PAD + ny], u.at[nx + 2:nx + 4, PAD:PAD + ny], ix - 1
            else:
                src, dst, to = u.at[nx:nx + 2, PAD:PAD + ny], u.at[0:2, PAD:PAD + ny], ix + 1
            return pltpu.make_async_remote_copy(
                src, dst, send_sem.at[k % 2, side], recv_sem.at[k % 2, side],
                device_id=(to, iy, iz), device_id_type=MESH)

        def ycopy(k, side, first=0, many=nx - 4, sem=2):
            to = iy - 1 if side == 0 else iy + 1
            part = pl.ds(first, many)
            return pltpu.make_async_remote_copy(
                ysend.at[k, side, part], yrecv.at[k, 1 - side, part], send_sem.at[k % 2, sem + side],
                recv_sem.at[k % 2, sem + side], device_id=(ix, to, iz), device_id_type=MESH)

        def corner(k, side):
            return ycopy(k, side, nx - 4, 4, 4)

        def place(x, rim):
            if not rim:
                return x - 2
            return x if x >= nx - 2 else nx - 4 + x

        def zcopy(k, n):
            src, dst = (rsend.at[k], rrecv.at[k]) if n == 2 else (zsend.at[k, n], zrecv.at[k, n])
            return pltpu.make_async_remote_copy(
                src, dst, zs_sem.at[k % 2, n], zr_sem.at[k % 2, n],
                device_id=(ix, iy, 1 - iz), device_id_type=MESH)

        def sending(spot, size, side):
            return spot > 0 if side == 0 else spot < size - 1

        def receiving(spot, size, side):
            return spot < size - 1 if side == 0 else spot > 0

        def sides(k):
            return (1,) if k == 2 else (0, 1)

        def each(make, k, spot, size, test, act):
            for side in sides(k):
                @pl.when(test(spot, size, side))
                def _():
                    act(make(k, side))

        def start_x(k):
            odd = lax.rem(ix, 2) == 1
            for side, turn in ((1, odd), (0, None), (1, jnp.logical_not(odd))):
                if side in sides(k):
                    go = sending(ix, ngx, side)
                    @pl.when(go if turn is None else go & turn)
                    def _():
                        xcopy(k, side).start()

        def start_y(k):
            each(ycopy, k, iy, ngy, sending, lambda c: c.start())

        def start_corner(k):
            each(corner, k, iy, ngy, sending, lambda c: c.start())

        def sent(k):
            each(xcopy, k, ix, ngx, sending, lambda c: c.wait_send())
            each(ycopy, k, iy, ngy, sending, lambda c: c.wait_send())
            each(corner, k, iy, ngy, sending, lambda c: c.wait_send())
            for n in range(3):
                zcopy(k, n).wait_send()

        def wait_y(k):
            each(ycopy, k, iy, ngy, receiving, lambda c: c.wait_recv())

        def wait_x(k):
            each(corner, k, iy, ngy, receiving, lambda c: c.wait_recv())
            each(xcopy, k, ix, ngx, receiving, lambda c: c.wait_recv())

        def along_z(k, values, rows):
            high, low = halves(values)
            lhs = jnp.concatenate([high, low], axis=1)
            found = jnp.dot(lhs, band[1 if k == 2 else 0], preferred_element_type=jnp.float32)
            return found[:, :nz].reshape(-1, rows, nz), found[:, nz:].reshape(-1, rows, nz)

        def picked(k, x, n, lo, hi, packed):
            rows = hi - lo
            values = us[k][pl.ds(x + 2, n), PAD + lo:PAD + hi, :].reshape(n * rows, nz)
            own, out = along_z(k, values, rows)
            zterm[pl.ds(x, n), lo:hi, :] = own
            for g in range(n):
                keep = jnp.concatenate([pair] * (rows // 8), axis=0) == x + g
                packed = jnp.where(keep, out[g], packed)
            return packed

        def rims_z(k):
            low = high = jnp.zeros((8, nz), jnp.float32)
            for h in range(2):
                low = picked(k, 2 + h * half, half, 0, 8, low)
                high = picked(k, 2 + h * half, half, ny - 8, ny, high)
            rsend[k, 0:8] = low
            rsend[k, 8:16] = high
            packed = jnp.zeros((ny, nz), jnp.float32)
            for at in (0, nx - 2):
                packed = picked(k, at, 2, 0, ny, packed)
            rsend[k, 16:16 + ny] = packed
            zcopy(k, 2).start()

        def put(k, x, slot, t, value):
            us[k][x + 2, PAD + t:PAD + t + 8, :] = value
            if t == 0:
                ysend[k, 0, slot] = value[0:2]
            if t == ny - 8:
                ysend[k, 1, slot] = value[6:8]

        def scale(x, n, tiles, t0, slot=None):
            for g in range(n):
                for t in tiles:
                    rows = slice(t, t + 8)
                    inv = 1.0 / (7.5 + d[x + g, rows])
                    rhs = b[x + g, rows]
                    value = inv * rhs
                    d[x + g, rows] = inv * (1.0 / 12.0)
                    b[x + g, rows] = 12.0 * rhs
                    put(0, x + g, x + g - 2 if slot is None else slot, t, value)
                    t0 = t0 + value * rhs
            return t0

        def shift_of(x):
            return jnp.bitwise_and(jnp.where(iz == 0, nz - 2, nz) - 2 * x, nz - 1)

        def stencil(k, x, n, tiles, source, carry, rim=False):
            u = us[k]
            for t in tiles:
                lo, hi = PAD + t, PAD + t + 8
                packed = source(t)
                line = [u[x + j, lo:hi, :] for j in range(n + 4 if k < 2 else n + 2)]
                for g in range(n):
                    at = x + g
                    rows = slice(t, t + 8)
                    c = line[g + 2]
                    z = zterm[at, rows] + jnp.where(
                        at_edge if k < 2 else at_upper, pltpu.roll(packed, shift_of(at), 1), 0.0)
                    if k < 2:
                        even, odd = carry
                        one = ((line[g + 1] + line[g + 3])
                               + (u[at + 2, lo - 1:hi - 1, :] + u[at + 2, lo + 1:hi + 1, :]))
                        two = ((line[g] + line[g + 4])
                               + (u[at + 2, lo - 2:hi - 2, :] + u[at + 2, lo + 2:hi + 2, :]))
                        w = (16.0 * one - two) + z
                        fresh = d[at, rows] * w
                        even = even + c * (b[at, rows] - w)
                        odd = odd + (c - fresh) * w
                        b[at, rows] = w
                        put(k + 1, at, place(at, rim), t, fresh)
                        carry = even, odd
                    else:
                        one = line[g + 1] + u[at + 2, lo - 1:hi - 1, :]
                        two = line[g] + u[at + 2, lo - 2:hi - 2, :]
                        w = (16.0 * one - two) + z
                        carry = carry + c * (b[at, rows] - (w + w))
            return carry

        def inside(k, make, carry):
            for h in range(2):
                zcopy(k, h).wait_recv()

                def chunk(i, state):
                    carry, packed = state
                    x = 2 + h * half + i * size
                    carry = make(h, x, carry)
                    if k < 2:
                        packed = picked(k + 1, x, size, 8, ny - 8, packed)
                    return carry, packed

                start = jnp.zeros((ny - 16, nz), jnp.float32)
                carry, packed = lax.fori_loop(0, half // size, chunk, (carry, start))
                if k < 2:
                    zsend[k + 1, h] = packed
                    zcopy(k + 1, h).start()
            return carry

        zero = jnp.zeros((8, nz), jnp.float32)

        loaded(b.at[0:8], 0)
        t0 = lax.fori_loop(0, 4, lambda n, c: scale(
            jnp.where(n < 2, n, nx - 4 + n), 1, full, c, nx - 4 + n), zero)
        hear(barrier, 1)
        start_x(0)
        start_corner(0)
        tell(known.at[0], hops[0])
        loaded(b.at[2:nx - 2, 0:32], 1)
        t0 = lax.fori_loop(0, (nx - 4) // strip, lambda n, c: scale(2 + n * strip, strip, ends, c), t0)
        start_y(0)
        rims_z(0)

        for h in range(2):
            packed = jnp.zeros((ny - 16, nz), jnp.float32)
            for n in range(LOADS):
                first = (h * LOADS + n) * piece
                loaded(b.at[0:2 * piece, 8:ny - 8], 2 + h * LOADS + n)
                run = divisor(piece, 15)

                def chunk(i, state):
                    t0, packed = state
                    x = 2 + first + i * run
                    t0 = scale(x, run, mid, t0)
                    return t0, picked(0, x, run, 8, ny - 8, packed)

                t0, packed = lax.fori_loop(0, piece // run, chunk, (t0, packed))
            zsend[0, h] = packed
            zcopy(0, h).start()

        def step(k, carry):
            if k:
                rims_z(k)

            def windows(h, x, carry):
                for n in range(0, size, window):
                    carry = stencil(k, x + n, window, mid, lambda t: zrecv[k, h, t - 8:t], carry)
                return carry

            carry = inside(k, windows, carry)
            wait_y(k)

            def row_in(x, slot):
                us[k][x + 2, PAD - 2:PAD, :] = yrecv[k, 0, slot]
                if k < 2:
                    us[k][x + 2, PAD + ny:PAD + ny + 2, :] = yrecv[k, 1, slot]

            @pl.loop(0, (nx - 4) // strip)
            def _(i):
                for g in range(strip):
                    row_in(2 + i * strip + g, i * strip + g)

            zcopy(k, 2).wait_recv()

            def border(i, carry):
                return stencil(k, 2 + i * border_run, border_run, ends,
                               lambda t: rrecv[k, 0:8] if t == 0 else rrecv[k, 8:16], carry)

            carry = lax.fori_loop(0, (nx - 4) // border_run, border, carry)
            if k == 1:
                sent(0)
            if k < 2:
                start_y(k + 1)
            wait_x(k)
            for x in (0, 1, nx - 2, nx - 1):
                row_in(x, place(x, True))
            for at in (0, nx - 2):
                carry = stencil(k, at, 2, full, lambda t: rrecv[k, 16 + t:24 + t], carry, True)
            if k < 2:
                start_x(k + 1)
                start_corner(k + 1)
            return carry

        hear(known.at[0], hops[0])
        tell(known.at[1], hops[1])
        s0, s1 = step(0, (zero, zero))
        for n in range(1, len(hops) - 1):
            hear(known.at[n], hops[n])
            tell(known.at[n + 1], hops[n + 1])
        s2, s3 = step(1, (zero, zero))

        owned = nx // ngy
        below = iy == ngy // 2 - 1
        above = iy == ngy // 2

        def fault_copy(which, to):
            return pltpu.make_async_remote_copy(
                fsend.at[:, pl.ds(to * owned, owned), :], frecv.at[which], fs_sem.at[to], fr_sem.at[which],
                device_id=(ix, to, iz), device_id_type=MESH)

        @pl.when(below | above)
        def _():
            edge = jnp.where(below, 1, 0)
            front = jnp.where(below, 1.0 / 24.0, 27.0 / 24.0)
            close = jnp.where(below, -27.0 / 24.0, -1.0 / 24.0)

            def term(x, slot):
                for j in range(3):
                    rows = ysend[j, edge, slot]
                    fsend[j, pl.ds(x, 1), :] = front * rows[0:1] + close * rows[1:2]

            @pl.loop(0, (nx - 4) // strip)
            def _(i):
                for g in range(strip):
                    term(2 + i * strip + g, i * strip + g)

            for x in (0, 1, nx - 2, nx - 1):
                term(x, place(x, True))

        for which, owner in enumerate((ngy // 2 - 1, ngy // 2)):
            @pl.when(iy == owner)
            def _():
                for to in range(ngy):
                    if to != owner:
                        fault_copy(which, to).start()
                frecv[which] = fsend[:, owner * owned:(owner + 1) * owned, :]

        slot = lax.broadcasted_iota(jnp.int32, (1, nz), 1)

        def spread(parts):
            spots = jnp.zeros((1, nz), jnp.float32)
            for j, part, by in parts:
                whole = jnp.sum(jnp.sum(part, axis=0, keepdims=True), axis=1, keepdims=True)
                spots = spots + jnp.where(slot == j, whole * by, 0.0)
            return spots

        unit = 1.0 / 12.0
        early = spread([(0, t0, 1.0), (1, s0, unit), (2, s1, unit), (3, s2, unit), (4, s3, unit)])
        s4 = step(2, zero)
        red[me] = early + spread([(5, s4, unit)])
        hear(known.at[len(hops) - 1], hops[-1])

        def sum_copy(who):
            return pltpu.make_async_remote_copy(
                red.at[me], red.at[me], rs_sem, rr_sem, device_id=who, device_id_type=MESH)

        others = [(x, y, z) for y in reversed(ys) for x in reversed(xs) for z in reversed(zs)][:-1]
        for who in others:
            sum_copy(who).start()

        for which, owner in enumerate((ngy // 2 - 1, ngy // 2)):
            @pl.when(iy != owner)
            def _():
                fault_copy(which, owner).wait_recv()
        sent(1)
        sent(2)
        for which, owner in enumerate((ngy // 2 - 1, ngy // 2)):
            @pl.when(iy == owner)
            def _():
                for to in range(ngy):
                    if to != owner:
                        fault_copy(which, to).wait_send()

        arrived = red.at[pl.ds(0, count - 1)]
        everyone = pltpu.make_async_remote_copy(
            arrived, arrived, rs_sem, rr_sem, device_id=others[0], device_id_type=MESH)
        everyone.wait_recv()
        sums = jnp.sum(red[...], axis=0)
        sums = [jnp.sum(jnp.where(slot == j, sums, 0.0), axis=1, keepdims=True) for j in range(6)]
        coefs = solve(sums[0], sums[1:])
        for j in range(3):
            coef_ref[j:j + 1, :] = jnp.broadcast_to(coefs[j], (1, nz))
        everyone.wait_send()

    return kernel


def blend(u0, u1, u2, coef_ref, fault, pre_ref, state_ref, norm_ref, out, slip, obuf, sbuf, out_sem):
    nx, ny, nz = obuf.shape
    coefs = [coef_ref[j:j + 1, :] for j in range(3)]

    def out_copy(c):
        part = pl.ds(c * CHUNK, CHUNK)
        return pltpu.make_async_copy(obuf.at[part], out.at[part], out_sem.at[c])

    slip_copy = pltpu.make_async_copy(sbuf, slip, out_sem.at[nx // CHUNK])

    def mixed(c):
        @pl.loop(0, CHUNK // 4)
        def _(i):
            for g in range(4):
                x = c * CHUNK + i * 4 + g
                for t in range(PAD, PAD + ny, 8):
                    rows = slice(t, t + 8)
                    obuf[x, t - PAD:t - PAD + 8] = (
                        coefs[0] * u0[x + 2, rows, :] + coefs[1] * u1[x + 2, rows, :]
                        + coefs[2] * u2[x + 2, rows, :])
        out_copy(c).start()

    mixed(0)
    traction = sum(coefs[j] * (fault[0, j] + fault[1, j]) for j in range(3))
    arg = (pre_ref[...] + 2.0 * traction) / norm_ref[...]
    half = jnp.float32(-0.6931471805599453)
    small = arg * (1.0 + arg * arg * (1.0 / 6.0) * (1.0 + arg * arg * 0.05))
    sinh = jnp.where(jnp.abs(arg) < 0.25, small, jnp.exp(arg + half) - jnp.exp(half - arg))
    sbuf[...] = jnp.exp(-state_ref[...]) * sinh
    slip_copy.start()
    pl.loop(1, nx // CHUNK)(mixed)
    slip_copy.wait()
    for c in range(nx // CHUNK):
        out_copy(c).wait()


def solution(mesh):
    sizes = tuple(mesh.shape[a] for a in AXES)
    assert sizes[1] % 2 == 0 and sizes[2] == 2

    def per_device(load, stiffness, prestress, state_var, normal_a):
        nx, ny, nz = load.shape
        assert nx % CHUNK == 0 and nx % 4 == 0 and 2 * nx <= nz and ny % 8 == 0 and ny >= 32
        f32 = jnp.float32
        count = sizes[0] * sizes[1] * sizes[2]
        padded = (nx + 4, ny + 2 * PAD, nz)
        vmem = pl.BlockSpec(memory_space=pltpu.VMEM)
        hbm = pl.BlockSpec(memory_space=pltpu.HBM)
        dma = pltpu.SemaphoreType.DMA
        u0, u1, u2, coefs, fault = pl.pallas_call(
            make_kernel(sizes),
            out_shape=(
                pltpu.VMEM(padded, f32),
                pltpu.VMEM(padded, f32),
                pltpu.VMEM(padded, f32),
                pltpu.VMEM((8, nz), f32),
                pltpu.VMEM((2, 3, nx // sizes[1], nz), f32),
            ),
            in_specs=[hbm, hbm],
            out_specs=(vmem,) * 5,
            scratch_shapes=[
                pltpu.VMEM((nx, ny, nz), f32),
                pltpu.VMEM((nx, ny, nz), f32),
                pltpu.VMEM((3, 2, nx, 2, nz), f32),
                pltpu.VMEM((3, 2, nx, 2, nz), f32),
                pltpu.VMEM((3, 2, ny - 16, nz), f32),
                pltpu.VMEM((3, 2, ny - 16, nz), f32),
                pltpu.VMEM((3, ny + 16, nz), f32),
                pltpu.VMEM((3, ny + 16, nz), f32),
                pltpu.VMEM((2, 2 * nz, 2 * nz), jnp.bfloat16),
                pltpu.VMEM((nx, ny, nz), f32),
                pltpu.VMEM((3, nx, nz), f32),
                pltpu.VMEM((count, 1, nz), f32),
                dma((2 + 2 * LOADS,)),
                dma((2, 6)),
                dma((2, 6)),
                dma((2, 3)),
                dma((2, 3)),
                dma((sizes[1],)),
                dma((2,)),
                dma,
                dma,
                pltpu.SemaphoreType.REGULAR((len(radii(sizes)),)),
            ],
            compiler_params=pltpu.CompilerParams(
                collective_id=0, has_side_effects=True, vmem_limit_bytes=54 * 2**20),
        )(load, stiffness)
        displacement, slip = pl.pallas_call(
            blend,
            out_shape=(
                jax.ShapeDtypeStruct(load.shape, f32),
                jax.ShapeDtypeStruct(prestress.shape, f32),
            ),
            in_specs=[vmem] * 8,
            out_specs=(hbm, hbm),
            scratch_shapes=[
                pltpu.VMEM((nx, ny, nz), f32),
                pltpu.VMEM(prestress.shape, f32),
                dma((nx // CHUNK + 1,)),
            ],
            compiler_params=pltpu.CompilerParams(vmem_limit_bytes=8 * 2**20),
        )(u0, u1, u2, coefs, fault, prestress, state_var, normal_a)
        return displacement, slip

    placed = (
        P("gx", "gy", "gz"),
        P("gx", "gy", "gz"),
        P(("gx", "gy"), "gz"),
        P(("gx", "gy"), "gz"),
        P(("gx", "gy"), "gz"),
    )
    return jax.shard_map(
        per_device,
        mesh=mesh,
        in_specs=placed,
        out_specs=(P("gx", "gy", "gz"), P(("gx", "gy"), "gz")),
        check_vma=False,
    )
```

time: 30.2 us -> 25.7 us (0.85)
  Pallas kernels: 29.3 us -> 24.8 us
    pallas_call x1, Pallas kernels: 27.2 us -> 23.4 us  [per_device(): pl.pallas_call(make_kernel(sizes), out_shape=(pltpu.VMEM(padded, f32), pl...]
    pallas_call x1, Pallas kernels: 2.08 us -> 1.44 us  [per_device(): pl.pallas_call(blend, out_shape=(jax.ShapeDtypeStruct(load.shape, f32), j...]
where the time goes in v2:
time: 25.7 us; the launch traced here: 25.5 us
  Pallas kernels  24.8 us (96%)
  between operations  0.69 us (3%)
    pallas_call x1, Pallas kernels, per_device(): pl.pallas_call(make_kernel(sizes), out_shape=(pltpu.VMEM(padded, f32), pl...  23.4 us
    pallas_call x1, Pallas kernels, per_device(): pl.pallas_call(blend, out_shape=(jax.ShapeDtypeStruct(load.shape, f32), j...  1.44 us

profile of v2, /device:TPU:0, one launch (start us, length us, event | category | flops | bytes accessed | tf_op | source)
XLA Modules:
  0.0 25.5 jit_solution(4909273950291701565)
XLA Ops:
  0.6 0.0 copy-start.2
  0.6 0.0 copy-start.1
  0.7 0.0 copy-start
  0.7 23.4 %shard_map.68 = (f32[68,80,128]{2,1,0:T(8,128)S(1)}, f32[68,80,128]{2,1,0:T(8,128)S(1)}, f32[68,80,128]{2,1,0:T(8,128)S(1)}, f32[8,128]{1,0:T(8,128)S(1)}, f32[2,3,16,128]{3,2,1,0:T(8,128)S(1)}) custom-call(f32[64,64,128]{2,1,0:T(8,128)} %load.1, f32[64,64,128]{2,1,0:T(8,128)} %stiff.1), custom_call_target="tpu_custom_call" | custom-call | tf_op jit(solution)/shard_map/pallas_call | solution.py:563
  24.1 0.0 copy-done.2
  24.1 0.0 copy-done.1
  24.1 0.0 copy-done
  24.1 1.4 %shard_map.69 = (f32[64,64,128]{2,1,0:T(8,128)}, f32[16,128]{1,0:T(8,128)}) custom-call(f32[68,80,128]{2,1,0:T(8,128)S(1)} %get-tuple-element.7.u0, f32[68,80,128]{2,1,0:T(8,128)S(1)} %get-tuple-element.8.u1, f32[68,80,128]{2,1,0:T(8,128)S(1)} %get-tuple-element.9.u2, f32[8,128]{1,0:T(8,128)S(1)} %get-tuple-element.10.coef_ref, ...), custom_call_target="tpu_custom_call" | custom-call | tf_op jit(solution)/shard_map/pallas_call | solution.py:601
Async XLA Ops:
  0.6 23.4 %copy-start.2 = (f32[16,128]{1,0:T(8,128)S(1)}, f32[16,128]{1,0:T(8,128)}, u32[]{:S(2)}) copy-start(f32[16,128]{1,0:T(8,128)} %norm_ref.1) | copy-start | bytes 24580
  0.6 23.4 %copy-start.1 = (f32[16,128]{1,0:T(8,128)S(1)}, f32[16,128]{1,0:T(8,128)}, u32[]{:S(2)}) copy-start(f32[16,128]{1,0:T(8,128)} %state_ref.1) | copy-start | bytes 24580
  0.7 23.4 %copy-start = (f32[16,128]{1,0:T(8,128)S(1)}, f32[16,128]{1,0:T(8,128)}, u32[]{:S(2)}) copy-start(f32[16,128]{1,0:T(8,128)} %pre_ref.1) | copy-start | bytes 24580

commit v3 on v2

--- a/solution.py
+++ b/solution.py
@@ -1,5 +1,3 @@
-import functools
-import itertools
 import jax
 import jax.numpy as jnp
 from jax import lax
@@ -11,7 +9,8 @@
 AXES = ("gx", "gy", "gz")
 PAD = 8
 CHUNK = 8
-LOADS = 2
+PIECES = 4
+EARLY = 1
 
 
 def total(values):
@@ -50,12 +49,10 @@
     return high, (values - high.astype(jnp.float32)).astype(jnp.bfloat16)
 
 
-def radii(sizes):
-    needed = sum(n - 1 for n in sizes)
-    hops, reached = [], 1
-    while reached < needed or len(hops) < 2:
-        hops.append(min(reached, max(needed - reached, 1)))
-        reached += hops[-1]
+def line_rounds(sizes):
+    hops = [1]
+    while 2 * hops[-1] < max(sizes[:2]) - 1:
+        hops.append(2 * hops[-1])
     return hops
 
 
@@ -65,18 +62,17 @@
 
     def kernel(load, stiff, u0, u1, u2, coef_ref, frecv,
                b, d, ysend, yrecv, zsend, zrecv, rsend, rrecv, band, zterm, fsend, red,
-               in_sem, send_sem, recv_sem, zs_sem, zr_sem, fs_sem, fr_sem, rs_sem, rr_sem,
+               in_sem, send_sem, x_sem, y_sem, z_sem, fr_sem, rs_sem, rr_sem,
                known):
         nx, ny, nz = b.shape
         us = (u0, u1, u2)
         ix, iy, iz = (lax.axis_index(a) for a in AXES)
         me = (ix * ngy + iy) * ngz + iz
         half = (nx - 4) // 2
-        size = divisor(half, 10)
-        window = divisor(size, 5)
-        piece = half // LOADS
-        strip = divisor(nx - 4, 6)
-        border_run = divisor(nx - 4, 30)
+        piece = (nx - 4) // PIECES
+        window = divisor(piece, 5)
+        run_y = divisor(half, 30)
+        strip = divisor(half, 6)
         mid = tuple(range(8, ny - 8, 8))
         ends = (0, ny - 8)
         full = tuple(range(0, ny, 8))
@@ -95,7 +91,7 @@
             for at in ends:
                 pltpu.make_async_copy(
                     src.at[2:nx - 2, at:at + 8], dst.at[2:nx - 2, at:at + 8], in_sem.at[1]).start()
-        for n in range(2 * LOADS):
+        for n in range(PIECES):
             part = pl.ds(2 + n * piece, piece)
             for src, dst in sources:
                 pltpu.make_async_copy(
@@ -105,28 +101,28 @@
             pltpu.make_async_copy(ref, ref, in_sem.at[n]).wait()
 
         barrier = pltpu.get_barrier_semaphore()
-        spots = (ix, iy, iz)
-
-        def ball(radius):
-            reach = [range(-min(radius, n - 1), min(radius, n - 1) + 1) for n in sizes]
-            for step in itertools.product(*reach):
-                if 0 < sum(abs(g) for g in step) <= radius:
-                    inside = [spot + g >= 0 if g < 0 else spot + g < n
-                              for spot, g, n in zip(spots, step, sizes) if g]
-                    yield functools.reduce(jnp.logical_and, inside), tuple(
-                        spot + g for spot, g in zip(spots, step))
-
-        def tell(sem, radius):
-            for there, who in ball(radius):
+        def lines(radius, axes=(0, 1)):
+            spots = (ix, iy, iz)
+            for axis in axes:
+                for gap in range(1, min(radius, sizes[axis] - 1) + 1):
+                    for step in (-gap, gap):
+                        to = spots[axis] + step
+                        yield (to >= 0 if step < 0 else to < sizes[axis],
+                               tuple(to if n == axis else spot for n, spot in enumerate(spots)))
+
+        def tell(sem, who):
+            for there, device in who:
                 @pl.when(there)
                 def _():
-                    pl.semaphore_signal(sem, inc=1, device_id=who, device_id_type=MESH)
-
-        def hear(sem, radius):
-            pl.semaphore_wait(sem, sum(jnp.where(there, 1, 0) for there, _ in ball(radius)))
-
-        hops = radii(sizes)
-        tell(barrier, 1)
+                    pl.semaphore_signal(sem, inc=1, device_id=device, device_id_type=MESH)
+
+        def hear(sem, who):
+            pl.semaphore_wait(sem, sum(jnp.where(there, 1, 0) for there, _ in who))
+
+        rounds = ([tuple(lines(hop)) for hop in line_rounds(sizes)]
+                  + [tuple(lines(ngy, (1,))), tuple(lines(ngz, (2,)))])
+        near = tuple(lines(1, (0, 1, 2)))
+        tell(barrier, near)
 
         zero_plane = jnp.zeros((2, ny, nz), jnp.float32)
         zero_rows = jnp.zeros((nx, 2, nz), jnp.float32)
@@ -165,25 +161,23 @@
         at_edge = (lane >= edge_low) & (lane < edge_low + 2)
         at_upper = at_edge & (iz == 1)
 
-        def xcopy(k, side):
+        def xcopy(k, n, side):
             u = us[k]
+            rows = pl.ds(PAD + n * (ny // 2), ny // 2)
             if side == 0:
-                src, dst, to = u.at[2:4, PAD:PAD + ny], u.at[nx + 2:nx + 4, PAD:PAD + ny], ix - 1
+                src, dst, to = u.at[2:4, rows], u.at[nx + 2:nx + 4, rows], ix - 1
             else:
-                src, dst, to = u.at[nx:nx + 2, PAD:PAD + ny], u.at[0:2, PAD:PAD + ny], ix + 1
+                src, dst, to = u.at[nx:nx + 2, rows], u.at[0:2, rows], ix + 1
             return pltpu.make_async_remote_copy(
-                src, dst, send_sem.at[k % 2, side], recv_sem.at[k % 2, side],
+                src, dst, send_sem, x_sem.at[k % 2, n, side],
                 device_id=(to, iy, iz), device_id_type=MESH)
 
-        def ycopy(k, side, first=0, many=nx - 4, sem=2):
+        def ycopy(k, n, side):
             to = iy - 1 if side == 0 else iy + 1
-            part = pl.ds(first, many)
+            part = pl.ds(n * half, half) if n < 2 else pl.ds(nx - 4, 4)
             return pltpu.make_async_remote_copy(
-                ysend.at[k, side, part], yrecv.at[k, 1 - side, part], send_sem.at[k % 2, sem + side],
-                recv_sem.at[k % 2, sem + side], device_id=(ix, to, iz), device_id_type=MESH)
-
-        def corner(k, side):
-            return ycopy(k, side, nx - 4, 4, 4)
+                ysend.at[k, side, part], yrecv.at[k, 1 - side, part], send_sem,
+                y_sem.at[k % 2, n, side], device_id=(ix, to, iz), device_id_type=MESH)
 
         def place(x, rim):
             if not rim:
@@ -191,9 +185,10 @@
             return x if x >= nx - 2 else nx - 4 + x
 
         def zcopy(k, n):
-            src, dst = (rsend.at[k], rrecv.at[k]) if n == 2 else (zsend.at[k, n], zrecv.at[k, n])
+            rim = isinstance(n, int) and n == PIECES
+            src, dst = (rsend.at[k], rrecv.at[k]) if rim else (zsend.at[k, n], zrecv.at[k, n])
             return pltpu.make_async_remote_copy(
-                src, dst, zs_sem.at[k % 2, n], zr_sem.at[k % 2, n],
+                src, dst, send_sem, z_sem.at[k % 2, n],
                 device_id=(ix, iy, 1 - iz), device_id_type=MESH)
 
         def sending(spot, size, side):
@@ -205,40 +200,37 @@
         def sides(k):
             return (1,) if k == 2 else (0, 1)
 
-        def each(make, k, spot, size, test, act):
+        def each(make, k, n, spot, size, test, act):
             for side in sides(k):
                 @pl.when(test(spot, size, side))
                 def _():
-                    act(make(k, side))
-
-        def start_x(k):
+                    act(make(k, n, side))
+
+        def start_x(k, n, core):
             odd = lax.rem(ix, 2) == 1
             for side, turn in ((1, odd), (0, None), (1, jnp.logical_not(odd))):
                 if side in sides(k):
-                    go = sending(ix, ngx, side)
+                    go = sending(ix, ngx, side) & (iz == core)
                     @pl.when(go if turn is None else go & turn)
                     def _():
-                        xcopy(k, side).start()
-
-        def start_y(k):
-            each(ycopy, k, iy, ngy, sending, lambda c: c.start())
-
-        def start_corner(k):
-            each(corner, k, iy, ngy, sending, lambda c: c.start())
+                        xcopy(k, n, side).start()
+
+        def start_y(k, n):
+            each(ycopy, k, n, iy, ngy, sending, lambda c: c.start())
+
+        def wait_y(k, n):
+            each(ycopy, k, n, iy, ngy, receiving, lambda c: c.wait_recv())
+
+        def wait_x(k, n):
+            each(xcopy, k, n, ix, ngx, receiving, lambda c: c.wait_recv())
 
         def sent(k):
-            each(xcopy, k, ix, ngx, sending, lambda c: c.wait_send())
-            each(ycopy, k, iy, ngy, sending, lambda c: c.wait_send())
-            each(corner, k, iy, ngy, sending, lambda c: c.wait_send())
             for n in range(3):
+                if n < 2:
+                    each(xcopy, k, n, ix, ngx, sending, lambda c: c.wait_send())
+                each(ycopy, k, n, iy, ngy, sending, lambda c: c.wait_send())
+            for n in range(PIECES + 1):
                 zcopy(k, n).wait_send()
-
-        def wait_y(k):
-            each(ycopy, k, iy, ngy, receiving, lambda c: c.wait_recv())
-
-        def wait_x(k):
-            each(corner, k, iy, ngy, receiving, lambda c: c.wait_recv())
-            each(xcopy, k, ix, ngx, receiving, lambda c: c.wait_recv())
 
         def along_z(k, values, rows):
             high, low = halves(values)
@@ -267,7 +259,7 @@
             for at in (0, nx - 2):
                 packed = picked(k, at, 2, 0, ny, packed)
             rsend[k, 16:16 + ny] = packed
-            zcopy(k, 2).start()
+            zcopy(k, PIECES).start()
 
         def put(k, x, slot, t, value):
             us[k][x + 2, PAD + t:PAD + t + 8, :] = value
@@ -324,106 +316,121 @@
                         carry = carry + c * (b[at, rows] - (w + w))
             return carry
 
-        def inside(k, make, carry):
-            for h in range(2):
-                zcopy(k, h).wait_recv()
-
-                def chunk(i, state):
-                    carry, packed = state
-                    x = 2 + h * half + i * size
-                    carry = make(h, x, carry)
-                    if k < 2:
-                        packed = picked(k + 1, x, size, 8, ny - 8, packed)
-                    return carry, packed
-
-                start = jnp.zeros((ny - 16, nz), jnp.float32)
-                carry, packed = lax.fori_loop(0, half // size, chunk, (carry, start))
+        def pack(k, n):
+            packed = picked(k, 2 + n * piece, piece, 8, ny - 8, jnp.zeros((ny - 16, nz), jnp.float32))
+            zsend[k, n] = packed
+            zcopy(k, n).start()
+
+        def inside(k, first, last, carry):
+            def part(n, carry):
+                zcopy(k, n).wait_recv()
+                x = 2 + n * piece
+                for g in range(0, piece, window):
+                    carry = stencil(k, x + g, window, mid, lambda t: zrecv[k, n, t - 8:t], carry)
                 if k < 2:
-                    zsend[k + 1, h] = packed
-                    zcopy(k + 1, h).start()
-            return carry
+                    pack(k + 1, n)
+                return carry
+
+            return lax.fori_loop(first, last, part, carry)
 
         zero = jnp.zeros((8, nz), jnp.float32)
 
         loaded(b.at[0:8], 0)
         t0 = lax.fori_loop(0, 4, lambda n, c: scale(
             jnp.where(n < 2, n, nx - 4 + n), 1, full, c, nx - 4 + n), zero)
-        hear(barrier, 1)
-        start_x(0)
-        start_corner(0)
-        tell(known.at[0], hops[0])
         loaded(b.at[2:nx - 2, 0:32], 1)
-        t0 = lax.fori_loop(0, (nx - 4) // strip, lambda n, c: scale(2 + n * strip, strip, ends, c), t0)
-        start_y(0)
+        for h in range(2):
+            t0 = lax.fori_loop(
+                0, half // strip, lambda n, c: scale(2 + h * half + n * strip, strip, ends, c), t0)
+            if h == 0:
+                hear(barrier, near)
+                for n in range(2):
+                    start_x(0, n, 0)
+                    start_x(0, n, 1)
+            start_y(0, h)
+        start_y(0, 2)
+        tell(known.at[0], rounds[0])
         rims_z(0)
 
-        for h in range(2):
-            packed = jnp.zeros((ny - 16, nz), jnp.float32)
-            for n in range(LOADS):
-                first = (h * LOADS + n) * piece
-                loaded(b.at[0:2 * piece, 8:ny - 8], 2 + h * LOADS + n)
-                run = divisor(piece, 15)
-
-                def chunk(i, state):
-                    t0, packed = state
-                    x = 2 + first + i * run
-                    t0 = scale(x, run, mid, t0)
-                    return t0, picked(0, x, run, 8, ny - 8, packed)
-
-                t0, packed = lax.fori_loop(0, piece // run, chunk, (t0, packed))
-            zsend[0, h] = packed
-            zcopy(0, h).start()
-
-        def step(k, carry):
-            if k:
-                rims_z(k)
-
-            def windows(h, x, carry):
-                for n in range(0, size, window):
-                    carry = stencil(k, x + n, window, mid, lambda t: zrecv[k, h, t - 8:t], carry)
-                return carry
-
-            carry = inside(k, windows, carry)
-            wait_y(k)
-
-            def row_in(x, slot):
+        def fresh_part(n, t0):
+            loaded(b.at[0:2 * piece, 8:ny - 8], 2 + n)
+            t0 = scale(2 + n * piece, piece, mid, t0)
+            pack(0, n)
+            return t0
+
+        def late_x(k):
+            for n in range(2):
+                start_x(k, n, 1)
+
+        t0 = lax.fori_loop(0, PIECES, fresh_part, t0)
+
+        def row_in(k, x, slot, side_set):
+            if 0 in side_set:
                 us[k][x + 2, PAD - 2:PAD, :] = yrecv[k, 0, slot]
-                if k < 2:
-                    us[k][x + 2, PAD + ny:PAD + ny + 2, :] = yrecv[k, 1, slot]
-
-            @pl.loop(0, (nx - 4) // strip)
+            if 1 in side_set and k < 2:
+                us[k][x + 2, PAD + ny:PAD + ny + 2, :] = yrecv[k, 1, slot]
+
+        def border(k, h, carry):
+            wait_y(k, h)
+
+            @pl.loop(0, half // strip)
             def _(i):
                 for g in range(strip):
-                    row_in(2 + i * strip + g, i * strip + g)
-
-            zcopy(k, 2).wait_recv()
-
-            def border(i, carry):
-                return stencil(k, 2 + i * border_run, border_run, ends,
+                    slot = h * half + i * strip + g
+                    row_in(k, slot + 2, slot, (0, 1))
+
+            def piece_of(i, carry):
+                return stencil(k, 2 + h * half + i * run_y, run_y, ends,
                                lambda t: rrecv[k, 0:8] if t == 0 else rrecv[k, 8:16], carry)
 
-            carry = lax.fori_loop(0, (nx - 4) // border_run, border, carry)
-            if k == 1:
-                sent(0)
+            carry = lax.fori_loop(0, half // run_y, piece_of, carry)
             if k < 2:
-                start_y(k + 1)
-            wait_x(k)
+                start_y(k + 1, h)
+            return carry
+
+        def outer(k, n, carry):
+            wait_x(k, n)
             for x in (0, 1, nx - 2, nx - 1):
-                row_in(x, place(x, True))
+                row_in(k, x, place(x, True), (n,))
             for at in (0, nx - 2):
-                carry = stencil(k, at, 2, full, lambda t: rrecv[k, 16 + t:24 + t], carry, True)
+                carry = stencil(k, at, 2, full[n * len(full) // 2:(n + 1) * len(full) // 2],
+                                lambda t: rrecv[k, 16 + t:24 + t], carry, True)
             if k < 2:
-                start_x(k + 1)
-                start_corner(k + 1)
+                start_x(k + 1, n, 0)
+                if k == 1:
+                    start_x(k + 1, n, 1)
             return carry
 
-        hear(known.at[0], hops[0])
-        tell(known.at[1], hops[1])
-        s0, s1 = step(0, (zero, zero))
-        for n in range(1, len(hops) - 1):
-            hear(known.at[n], hops[n])
-            tell(known.at[n + 1], hops[n + 1])
-        s2, s3 = step(1, (zero, zero))
+        def borders(k, carry):
+            zcopy(k, PIECES).wait_recv()
+            for h in range(2):
+                carry = border(k, h, carry)
+            wait_y(k, 2)
+            return carry
+
+        def pass_on(n):
+            hear(known.at[n], rounds[n])
+            if n + 1 < len(rounds):
+                tell(known.at[n + 1], rounds[n + 1])
+
+        lead = PIECES - 1
+        state = inside(0, 0, lead, (zero, zero))
+        for n in range(len(rounds) - 3):
+            pass_on(n)
+        state = borders(0, state)
+        state = outer(0, 1, outer(0, 0, state))
+        start_y(1, 2)
+        s0, s1 = inside(0, lead, PIECES, state)
+        late_x(1)
+        rims_z(1)
+        state = inside(1, 0, lead, (zero, zero))
+        pass_on(len(rounds) - 3)
+        state = borders(1, state)
+        state = outer(1, 0, state)
+        state = inside(1, lead, PIECES, state)
+        s2, s3 = outer(1, 1, state)
+        start_y(2, 2)
+        rims_z(2)
 
         owned = nx // ngy
         below = iy == ngy // 2 - 1
@@ -431,7 +438,7 @@
 
         def fault_copy(which, to):
             return pltpu.make_async_remote_copy(
-                fsend.at[:, pl.ds(to * owned, owned), :], frecv.at[which], fs_sem.at[to], fr_sem.at[which],
+                fsend.at[:, pl.ds(to * owned, owned), :], frecv.at[which], send_sem, fr_sem.at[which],
                 device_id=(ix, to, iz), device_id_type=MESH)
 
         @pl.when(below | above)
@@ -472,9 +479,12 @@
 
         unit = 1.0 / 12.0
         early = spread([(0, t0, 1.0), (1, s0, unit), (2, s1, unit), (3, s2, unit), (4, s3, unit)])
-        s4 = step(2, zero)
+        s4 = inside(2, 0, PIECES, zero)
+        s4 = borders(2, s4)
+        pass_on(len(rounds) - 2)
+        s4 = outer(2, 1, outer(2, 0, s4))
         red[me] = early + spread([(5, s4, unit)])
-        hear(known.at[len(hops) - 1], hops[-1])
+        hear(known.at[len(rounds) - 1], rounds[-1])
 
         def sum_copy(who):
             return pltpu.make_async_remote_copy(
@@ -488,8 +498,8 @@
             @pl.when(iy != owner)
             def _():
                 fault_copy(which, owner).wait_recv()
-        sent(1)
-        sent(2)
+        for k in range(3):
+            sent(k)
         for which, owner in enumerate((ngy // 2 - 1, ngy // 2)):
             @pl.when(iy == owner)
             def _():
@@ -553,7 +563,7 @@
 
     def per_device(load, stiffness, prestress, state_var, normal_a):
         nx, ny, nz = load.shape
-        assert nx % CHUNK == 0 and nx % 4 == 0 and 2 * nx <= nz and ny % 8 == 0 and ny >= 32
+        assert nx % CHUNK == 0 and nx % 4 == 0 and 2 * nx <= nz and (nx - 4) % PIECES == 0 and ny % 8 == 0 and ny >= 32
         f32 = jnp.float32
         count = sizes[0] * sizes[1] * sizes[2]
         padded = (nx + 4, ny + 2 * PAD, nz)
@@ -576,24 +586,23 @@
                 pltpu.VMEM((nx, ny, nz), f32),
                 pltpu.VMEM((3, 2, nx, 2, nz), f32),
                 pltpu.VMEM((3, 2, nx, 2, nz), f32),
-                pltpu.VMEM((3, 2, ny - 16, nz), f32),
-                pltpu.VMEM((3, 2, ny - 16, nz), f32),
+                pltpu.VMEM((3, PIECES, ny - 16, nz), f32),
+                pltpu.VMEM((3, PIECES, ny - 16, nz), f32),
                 pltpu.VMEM((3, ny + 16, nz), f32),
                 pltpu.VMEM((3, ny + 16, nz), f32),
                 pltpu.VMEM((2, 2 * nz, 2 * nz), jnp.bfloat16),
                 pltpu.VMEM((nx, ny, nz), f32),
                 pltpu.VMEM((3, nx, nz), f32),
                 pltpu.VMEM((count, 1, nz), f32),
-                dma((2 + 2 * LOADS,)),
-                dma((2, 6)),
-                dma((2, 6)),
-                dma((2, 3)),
-                dma((2, 3)),
-                dma((sizes[1],)),
+                dma((2 + PIECES,)),
+                dma,
+                dma((2, 2, 2)),
+                dma((2, 3, 2)),
+                dma((2, PIECES + 1)),
                 dma((2,)),
                 dma,
                 dma,
-                pltpu.SemaphoreType.REGULAR((len(radii(sizes)),)),
+                pltpu.SemaphoreType.REGULAR((len(line_rounds(sizes)) + 2,)),
             ],
             compiler_params=pltpu.CompilerParams(
                 collective_id=0, has_side_effects=True, vmem_limit_bytes=54 * 2**20),

time: 25.7 us -> 24.6 us (0.957)
  Pallas kernels: 24.8 us -> 23.7 us
    pallas_call x1, Pallas kernels: 23.4 us -> 22.3 us  [per_device(): pl.pallas_call(make_kernel(sizes), out_shape=(pltpu.VMEM(padded, f32), pl...]
where the time goes in v3:
time: 24.6 us; the launch traced here: 24.4 us
  Pallas kernels  23.7 us (96%)
  between operations  0.69 us (3%)
    pallas_call x1, Pallas kernels, per_device(): pl.pallas_call(make_kernel(sizes), out_shape=(pltpu.VMEM(padded, f32), pl...  22.3 us
    pallas_call x1, Pallas kernels, per_device(): pl.pallas_call(blend, out_shape=(jax.ShapeDtypeStruct(load.shape, f32), j...  1.44 us

profile of v3, /device:TPU:0, one launch (start us, length us, event | category | flops | bytes accessed | tf_op | source)
XLA Modules:
  0.0 24.4 jit_solution(15650686637874333784)
XLA Ops:
  0.6 0.0 copy-start.2
  0.6 0.0 copy-start.1
  0.7 0.0 copy-start
  0.7 22.3 %shard_map.68 = (f32[68,80,128]{2,1,0:T(8,128)S(1)}, f32[68,80,128]{2,1,0:T(8,128)S(1)}, f32[68,80,128]{2,1,0:T(8,128)S(1)}, f32[8,128]{1,0:T(8,128)S(1)}, f32[2,3,16,128]{3,2,1,0:T(8,128)S(1)}) custom-call(f32[64,64,128]{2,1,0:T(8,128)} %load.1, f32[64,64,128]{2,1,0:T(8,128)} %stiff.1), custom_call_target="tpu_custom_call" | custom-call | tf_op jit(solution)/shard_map/pallas_call | solution.py:573
  22.9 0.0 copy-done.2
  22.9 0.0 copy-done.1
  23.0 0.0 copy-done
  23.0 1.4 %shard_map.69 = (f32[64,64,128]{2,1,0:T(8,128)}, f32[16,128]{1,0:T(8,128)}) custom-call(f32[68,80,128]{2,1,0:T(8,128)S(1)} %get-tuple-element.7.u0, f32[68,80,128]{2,1,0:T(8,128)S(1)} %get-tuple-element.8.u1, f32[68,80,128]{2,1,0:T(8,128)S(1)} %get-tuple-element.9.u2, f32[8,128]{1,0:T(8,128)S(1)} %get-tuple-element.10.coef_ref, ...), custom_call_target="tpu_custom_call" | custom-call | tf_op jit(solution)/shard_map/pallas_call | solution.py:610
Async XLA Ops:
  0.6 22.3 %copy-start.2 = (f32[16,128]{1,0:T(8,128)S(1)}, f32[16,128]{1,0:T(8,128)}, u32[]{:S(2)}) copy-start(f32[16,128]{1,0:T(8,128)} %norm_ref.1) | copy-start | bytes 24580
  0.6 22.3 %copy-start.1 = (f32[16,128]{1,0:T(8,128)S(1)}, f32[16,128]{1,0:T(8,128)}, u32[]{:S(2)}) copy-start(f32[16,128]{1,0:T(8,128)} %state_ref.1) | copy-start | bytes 24580
  0.7 22.3 %copy-start = (f32[16,128]{1,0:T(8,128)S(1)}, f32[16,128]{1,0:T(8,128)}, u32[]{:S(2)}) copy-start(f32[16,128]{1,0:T(8,128)} %pre_ref.1) | copy-start | bytes 24580

commit v4 on v3

--- a/solution.py
+++ b/solution.py
@@ -10,7 +10,6 @@
 PAD = 8
 CHUNK = 8
 PIECES = 4
-EARLY = 1
 
 
 def total(values):
@@ -62,7 +61,8 @@
 
     def kernel(load, stiff, u0, u1, u2, coef_ref, frecv,
                b, d, ysend, yrecv, zsend, zrecv, rsend, rrecv, band, zterm, fsend, red,
-               in_sem, send_sem, x_sem, y_sem, z_sem, fr_sem, rs_sem, rr_sem,
+               dhalo, qsend, qhalo,
+               in_sem, send_sem, x_sem, y_sem, z_sem, fr_sem, rs_sem, rr_sem, q_sem,
                known):
         nx, ny, nz = b.shape
         us = (u0, u1, u2)
@@ -161,15 +161,15 @@
         at_edge = (lane >= edge_low) & (lane < edge_low + 2)
         at_upper = at_edge & (iz == 1)
 
-        def xcopy(k, n, side):
+        def xcopy(k, side):
             u = us[k]
-            rows = pl.ds(PAD + n * (ny // 2), ny // 2)
+            rows = pl.ds(PAD, ny)
             if side == 0:
                 src, dst, to = u.at[2:4, rows], u.at[nx + 2:nx + 4, rows], ix - 1
             else:
                 src, dst, to = u.at[nx:nx + 2, rows], u.at[0:2, rows], ix + 1
             return pltpu.make_async_remote_copy(
-                src, dst, send_sem, x_sem.at[k % 2, n, side],
+                src, dst, send_sem, x_sem.at[k, side],
                 device_id=(to, iy, iz), device_id_type=MESH)
 
         def ycopy(k, n, side):
@@ -198,7 +198,17 @@
             return spot < size - 1 if side == 0 else spot > 0
 
         def sides(k):
-            return (1,) if k == 2 else (0, 1)
+            return (0,) if k == 2 else (0, 1)
+
+        def d_copy():
+            return pltpu.make_async_remote_copy(
+                d.at[nx - 2:nx], dhalo, send_sem, q_sem.at[0],
+                device_id=(ix + 1, iy, iz), device_id_type=MESH)
+
+        def q_copy():
+            return pltpu.make_async_remote_copy(
+                qsend, qhalo, send_sem, q_sem.at[1],
+                device_id=(ix + 1, iy, iz), device_id_type=MESH)
 
         def each(make, k, n, spot, size, test, act):
             for side in sides(k):
@@ -206,14 +216,13 @@
                 def _():
                     act(make(k, n, side))
 
-        def start_x(k, n, core):
+        def start_x(k):
             odd = lax.rem(ix, 2) == 1
             for side, turn in ((1, odd), (0, None), (1, jnp.logical_not(odd))):
-                if side in sides(k):
-                    go = sending(ix, ngx, side) & (iz == core)
-                    @pl.when(go if turn is None else go & turn)
-                    def _():
-                        xcopy(k, n, side).start()
+                go = sending(ix, ngx, side)
+                @pl.when(go if turn is None else go & turn)
+                def _():
+                    xcopy(k, side).start()
 
         def start_y(k, n):
             each(ycopy, k, n, iy, ngy, sending, lambda c: c.start())
@@ -221,13 +230,13 @@
         def wait_y(k, n):
             each(ycopy, k, n, iy, ngy, receiving, lambda c: c.wait_recv())
 
-        def wait_x(k, n):
-            each(xcopy, k, n, ix, ngx, receiving, lambda c: c.wait_recv())
+        def wait_x(k, n=0):
+            each(lambda k, n, side: xcopy(k, side), k, n, ix, ngx, receiving, lambda c: c.wait_recv())
 
         def sent(k):
             for n in range(3):
-                if n < 2:
-                    each(xcopy, k, n, ix, ngx, sending, lambda c: c.wait_send())
+                if n == 0 and k < 2:
+                    each(lambda k, n, side: xcopy(k, side), k, n, ix, ngx, sending, lambda c: c.wait_send())
                 each(ycopy, k, n, iy, ngy, sending, lambda c: c.wait_send())
             for n in range(PIECES + 1):
                 zcopy(k, n).wait_send()
@@ -310,8 +319,8 @@
                         put(k + 1, at, place(at, rim), t, fresh)
                         carry = even, odd
                     else:
-                        one = line[g + 1] + u[at + 2, lo - 1:hi - 1, :]
-                        two = line[g] + u[at + 2, lo - 2:hi - 2, :]
+                        one = line[g + 1] + u[at + 2, lo + 1:hi + 1, :]
+                        two = line[g] + u[at + 2, lo + 2:hi + 2, :]
                         w = (16.0 * one - two) + z
                         carry = carry + c * (b[at, rows] - (w + w))
             return carry
@@ -344,9 +353,7 @@
                 0, half // strip, lambda n, c: scale(2 + h * half + n * strip, strip, ends, c), t0)
             if h == 0:
                 hear(barrier, near)
-                for n in range(2):
-                    start_x(0, n, 0)
-                    start_x(0, n, 1)
+                start_x(0)
             start_y(0, h)
         start_y(0, 2)
         tell(known.at[0], rounds[0])
@@ -358,16 +365,12 @@
             pack(0, n)
             return t0
 
-        def late_x(k):
-            for n in range(2):
-                start_x(k, n, 1)
-
         t0 = lax.fori_loop(0, PIECES, fresh_part, t0)
 
         def row_in(k, x, slot, side_set):
-            if 0 in side_set:
+            if 0 in side_set and k < 2:
                 us[k][x + 2, PAD - 2:PAD, :] = yrecv[k, 0, slot]
-            if 1 in side_set and k < 2:
+            if 1 in side_set:
                 us[k][x + 2, PAD + ny:PAD + ny + 2, :] = yrecv[k, 1, slot]
 
         def border(k, h, carry):
@@ -389,17 +392,49 @@
             return carry
 
         def outer(k, n, carry):
-            wait_x(k, n)
             for x in (0, 1, nx - 2, nx - 1):
                 row_in(k, x, place(x, True), (n,))
             for at in (0, nx - 2):
                 carry = stencil(k, at, 2, full[n * len(full) // 2:(n + 1) * len(full) // 2],
                                 lambda t: rrecv[k, 16 + t:24 + t], carry, True)
-            if k < 2:
-                start_x(k + 1, n, 0)
-                if k == 1:
-                    start_x(k + 1, n, 1)
             return carry
+
+        def lacking():
+            for x in (0, 1, nx - 2, nx - 1):
+                row_in(1, x, place(x, True), (0, 1))
+
+            @pl.when(ix < ngx - 1)
+            def _():
+                at = nx - 2
+                for t in full:
+                    lo, hi = PAD + t, PAD + t + 8
+                    line = [u1[at + j, lo:hi, :] for j in range(4)]
+                    for g in range(2):
+                        z = zterm[at + g, t:t + 8] + jnp.where(
+                            at_edge, pltpu.roll(rrecv[1, 16 + t:24 + t], shift_of(at + g), 1), 0.0)
+                        one = line[g + 1] + (u1[at + g + 2, lo - 1:hi - 1, :] + u1[at + g + 2, lo + 1:hi + 1, :])
+                        two = line[g] + (u1[at + g + 2, lo - 2:hi - 2, :] + u1[at + g + 2, lo + 2:hi + 2, :])
+                        if g == 0:
+                            one = one + line[3]
+                        qsend[g, t:t + 8] = (16.0 * one - two) + z
+                q_copy().start()
+
+        def last_planes(carry):
+            for x in (0, 1, nx - 2, nx - 1):
+                row_in(2, x, place(x, True), (1,))
+            carry = stencil(2, nx - 2, 2, full, lambda t: rrecv[2, 16 + t:24 + t], carry, True)
+
+            @pl.when(ix > 0)
+            def _():
+                d_copy().wait_recv()
+                q_copy().wait_recv()
+                for t in full:
+                    rows, lines = slice(t, t + 8), slice(PAD + t, PAD + t + 8)
+                    first, second = u1[2, lines, :], u1[3, lines, :]
+                    u2[1, lines, :] = dhalo[1, rows] * (qhalo[1, rows] + (16.0 * first - second))
+                    u2[0, lines, :] = dhalo[0, rows] * (qhalo[0, rows] - first)
+
+            return stencil(2, 0, 2, full, lambda t: rrecv[2, 16 + t:24 + t], carry, True)
 
         def borders(k, carry):
             zcopy(k, PIECES).wait_recv()
@@ -413,23 +448,30 @@
             if n + 1 < len(rounds):
                 tell(known.at[n + 1], rounds[n + 1])
 
+        @pl.when(ix < ngx - 1)
+        def _():
+            d_copy().start()
+
         lead = PIECES - 1
         state = inside(0, 0, lead, (zero, zero))
         for n in range(len(rounds) - 3):
             pass_on(n)
         state = borders(0, state)
+        wait_x(0)
         state = outer(0, 1, outer(0, 0, state))
+        start_x(1)
         start_y(1, 2)
         s0, s1 = inside(0, lead, PIECES, state)
-        late_x(1)
         rims_z(1)
         state = inside(1, 0, lead, (zero, zero))
         pass_on(len(rounds) - 3)
         state = borders(1, state)
+        lacking()
+        state = inside(1, lead, PIECES, state)
+        wait_x(1)
         state = outer(1, 0, state)
-        state = inside(1, lead, PIECES, state)
+        start_y(2, 2)
         s2, s3 = outer(1, 1, state)
-        start_y(2, 2)
         rims_z(2)
 
         owned = nx // ngy
@@ -482,7 +524,7 @@
         s4 = inside(2, 0, PIECES, zero)
         s4 = borders(2, s4)
         pass_on(len(rounds) - 2)
-        s4 = outer(2, 1, outer(2, 0, s4))
+        s4 = last_planes(s4)
         red[me] = early + spread([(5, s4, unit)])
         hear(known.at[len(rounds) - 1], rounds[-1])
 
@@ -500,6 +542,11 @@
                 fault_copy(which, owner).wait_recv()
         for k in range(3):
             sent(k)
+
+        @pl.when(ix < ngx - 1)
+        def _():
+            d_copy().wait_send()
+            q_copy().wait_send()
         for which, owner in enumerate((ngy // 2 - 1, ngy // 2)):
             @pl.when(iy == owner)
             def _():
@@ -594,14 +641,18 @@
                 pltpu.VMEM((nx, ny, nz), f32),
                 pltpu.VMEM((3, nx, nz), f32),
                 pltpu.VMEM((count, 1, nz), f32),
+                pltpu.VMEM((2, ny, nz), f32),
+                pltpu.VMEM((2, ny, nz), f32),
+                pltpu.VMEM((2, ny, nz), f32),
                 dma((2 + PIECES,)),
                 dma,
-                dma((2, 2, 2)),
+                dma((2, 2)),
                 dma((2, 3, 2)),
                 dma((2, PIECES + 1)),
                 dma((2,)),
                 dma,
                 dma,
+                dma((2,)),
                 pltpu.SemaphoreType.REGULAR((len(line_rounds(sizes)) + 2,)),
             ],
             compiler_params=pltpu.CompilerParams(

time: 24.6 us -> 23.8 us (0.967)
  Pallas kernels: 23.7 us -> 23 us
    pallas_call x1, Pallas kernels: 22.3 us -> 21.5 us  [per_device(): pl.pallas_call(make_kernel(sizes), out_shape=(pltpu.VMEM(padded, f32), pl...]
where the time goes in v4:
time: 23.8 us; the launch traced here: 23.7 us
  Pallas kernels  23 us (97%)
  between operations  0.69 us (3%)
    pallas_call x1, Pallas kernels, per_device(): pl.pallas_call(make_kernel(sizes), out_shape=(pltpu.VMEM(padded, f32), pl...  21.5 us
    pallas_call x1, Pallas kernels, per_device(): pl.pallas_call(blend, out_shape=(jax.ShapeDtypeStruct(load.shape, f32), j...  1.44 us

profile of v4, /device:TPU:0, one launch (start us, length us, event | category | flops | bytes accessed | tf_op | source)
XLA Modules:
  0.0 23.7 jit_solution(4581251175745448925)
XLA Ops:
  0.6 0.0 copy-start.2
  0.6 0.0 copy-start.1
  0.7 0.0 copy-start
  0.7 21.5 %shard_map.68 = (f32[68,80,128]{2,1,0:T(8,128)S(1)}, f32[68,80,128]{2,1,0:T(8,128)S(1)}, f32[68,80,128]{2,1,0:T(8,128)S(1)}, f32[8,128]{1,0:T(8,128)S(1)}, f32[2,3,16,128]{3,2,1,0:T(8,128)S(1)}) custom-call(f32[64,64,128]{2,1,0:T(8,128)} %load.1, f32[64,64,128]{2,1,0:T(8,128)} %stiff.1), custom_call_target="tpu_custom_call" | custom-call | tf_op jit(solution)/shard_map/pallas_call | solution.py:620
  22.2 0.0 copy-done.2
  22.2 0.0 copy-done.1
  22.2 0.0 copy-done
  22.2 1.4 %shard_map.69 = (f32[64,64,128]{2,1,0:T(8,128)}, f32[16,128]{1,0:T(8,128)}) custom-call(f32[68,80,128]{2,1,0:T(8,128)S(1)} %get-tuple-element.7.u0, f32[68,80,128]{2,1,0:T(8,128)S(1)} %get-tuple-element.8.u1, f32[68,80,128]{2,1,0:T(8,128)S(1)} %get-tuple-element.9.u2, f32[8,128]{1,0:T(8,128)S(1)} %get-tuple-element.10.coef_ref, ...), custom_call_target="tpu_custom_call" | custom-call | tf_op jit(solution)/shard_map/pallas_call | solution.py:661
Async XLA Ops:
  0.6 21.6 %copy-start.2 = (f32[16,128]{1,0:T(8,128)S(1)}, f32[16,128]{1,0:T(8,128)}, u32[]{:S(2)}) copy-start(f32[16,128]{1,0:T(8,128)} %norm_ref.1) | copy-start | bytes 24580
  0.6 21.6 %copy-start.1 = (f32[16,128]{1,0:T(8,128)S(1)}, f32[16,128]{1,0:T(8,128)}, u32[]{:S(2)}) copy-start(f32[16,128]{1,0:T(8,128)} %state_ref.1) | copy-start | bytes 24580
  0.7 21.6 %copy-start = (f32[16,128]{1,0:T(8,128)S(1)}, f32[16,128]{1,0:T(8,128)}, u32[]{:S(2)}) copy-start(f32[16,128]{1,0:T(8,128)} %pre_ref.1) | copy-start | bytes 24580

commit v5 on v4

--- a/solution.py
+++ b/solution.py
@@ -202,13 +202,13 @@
 
         def d_copy():
             return pltpu.make_async_remote_copy(
-                d.at[nx - 2:nx], dhalo, send_sem, q_sem.at[0],
-                device_id=(ix + 1, iy, iz), device_id_type=MESH)
+                d.at[0:2], dhalo, send_sem, q_sem.at[0],
+                device_id=(ix - 1, iy, iz), device_id_type=MESH)
 
         def q_copy():
             return pltpu.make_async_remote_copy(
                 qsend, qhalo, send_sem, q_sem.at[1],
-                device_id=(ix + 1, iy, iz), device_id_type=MESH)
+                device_id=(ix - 1, iy, iz), device_id_type=MESH)
 
         def each(make, k, n, spot, size, test, act):
             for side in sides(k):
@@ -298,7 +298,7 @@
             for t in tiles:
                 lo, hi = PAD + t, PAD + t + 8
                 packed = source(t)
-                line = [u[x + j, lo:hi, :] for j in range(n + 4 if k < 2 else n + 2)]
+                line = [u[x + j, lo:hi, :] if k < 2 or j > 1 else None for j in range(n + 4)]
                 for g in range(n):
                     at = x + g
                     rows = slice(t, t + 8)
@@ -319,8 +319,8 @@
                         put(k + 1, at, place(at, rim), t, fresh)
                         carry = even, odd
                     else:
-                        one = line[g + 1] + u[at + 2, lo + 1:hi + 1, :]
-                        two = line[g] + u[at + 2, lo + 2:hi + 2, :]
+                        one = line[g + 3] + u[at + 2, lo + 1:hi + 1, :]
+                        two = line[g + 4] + u[at + 2, lo + 2:hi + 2, :]
                         w = (16.0 * one - two) + z
                         carry = carry + c * (b[at, rows] - (w + w))
             return carry
@@ -403,38 +403,37 @@
             for x in (0, 1, nx - 2, nx - 1):
                 row_in(1, x, place(x, True), (0, 1))
 
-            @pl.when(ix < ngx - 1)
-            def _():
-                at = nx - 2
+            @pl.when(ix > 0)
+            def _():
                 for t in full:
                     lo, hi = PAD + t, PAD + t + 8
-                    line = [u1[at + j, lo:hi, :] for j in range(4)]
+                    line = [u1[j + 2, lo:hi, :] for j in range(4)]
                     for g in range(2):
-                        z = zterm[at + g, t:t + 8] + jnp.where(
-                            at_edge, pltpu.roll(rrecv[1, 16 + t:24 + t], shift_of(at + g), 1), 0.0)
-                        one = line[g + 1] + (u1[at + g + 2, lo - 1:hi - 1, :] + u1[at + g + 2, lo + 1:hi + 1, :])
-                        two = line[g] + (u1[at + g + 2, lo - 2:hi - 2, :] + u1[at + g + 2, lo + 2:hi + 2, :])
-                        if g == 0:
-                            one = one + line[3]
+                        z = zterm[g, t:t + 8] + jnp.where(
+                            at_edge, pltpu.roll(rrecv[1, 16 + t:24 + t], shift_of(g), 1), 0.0)
+                        one = line[g + 1] + (u1[g + 2, lo - 1:hi - 1, :] + u1[g + 2, lo + 1:hi + 1, :])
+                        two = line[g + 2] + (u1[g + 2, lo - 2:hi - 2, :] + u1[g + 2, lo + 2:hi + 2, :])
+                        if g == 1:
+                            one = one + line[0]
                         qsend[g, t:t + 8] = (16.0 * one - two) + z
                 q_copy().start()
 
         def last_planes(carry):
             for x in (0, 1, nx - 2, nx - 1):
                 row_in(2, x, place(x, True), (1,))
-            carry = stencil(2, nx - 2, 2, full, lambda t: rrecv[2, 16 + t:24 + t], carry, True)
-
-            @pl.when(ix > 0)
+            carry = stencil(2, 0, 2, full, lambda t: rrecv[2, 16 + t:24 + t], carry, True)
+
+            @pl.when(ix < ngx - 1)
             def _():
                 d_copy().wait_recv()
                 q_copy().wait_recv()
                 for t in full:
                     rows, lines = slice(t, t + 8), slice(PAD + t, PAD + t + 8)
-                    first, second = u1[2, lines, :], u1[3, lines, :]
-                    u2[1, lines, :] = dhalo[1, rows] * (qhalo[1, rows] + (16.0 * first - second))
-                    u2[0, lines, :] = dhalo[0, rows] * (qhalo[0, rows] - first)
-
-            return stencil(2, 0, 2, full, lambda t: rrecv[2, 16 + t:24 + t], carry, True)
+                    first, second = u1[nx + 1, lines, :], u1[nx, lines, :]
+                    u2[nx + 2, lines, :] = dhalo[0, rows] * (qhalo[0, rows] + (16.0 * first - second))
+                    u2[nx + 3, lines, :] = dhalo[1, rows] * (qhalo[1, rows] - first)
+
+            return stencil(2, nx - 2, 2, full, lambda t: rrecv[2, 16 + t:24 + t], carry, True)
 
         def borders(k, carry):
             zcopy(k, PIECES).wait_recv()
@@ -448,7 +447,7 @@
             if n + 1 < len(rounds):
                 tell(known.at[n + 1], rounds[n + 1])
 
-        @pl.when(ix < ngx - 1)
+        @pl.when(ix > 0)
         def _():
             d_copy().start()
 
@@ -522,8 +521,8 @@
         unit = 1.0 / 12.0
         early = spread([(0, t0, 1.0), (1, s0, unit), (2, s1, unit), (3, s2, unit), (4, s3, unit)])
         s4 = inside(2, 0, PIECES, zero)
+        pass_on(len(rounds) - 2)
         s4 = borders(2, s4)
-        pass_on(len(rounds) - 2)
         s4 = last_planes(s4)
         red[me] = early + spread([(5, s4, unit)])
         hear(known.at[len(rounds) - 1], rounds[-1])
@@ -543,7 +542,7 @@
         for k in range(3):
             sent(k)
 
-        @pl.when(ix < ngx - 1)
+        @pl.when(ix > 0)
         def _():
             d_copy().wait_send()
             q_copy().wait_send()

time: 23.8 us -> 23.8 us (level)
  no operation moved by 1% of the time
where the time goes in v5:
time: 23.8 us; the launch traced here: 23.7 us
  Pallas kernels  23 us (97%)
  between operations  0.69 us (3%)
    pallas_call x1, Pallas kernels, per_device(): pl.pallas_call(make_kernel(sizes), out_shape=(pltpu.VMEM(padded, f32), pl...  21.5 us
    pallas_call x1, Pallas kernels, per_device(): pl.pallas_call(blend, out_shape=(jax.ShapeDtypeStruct(load.shape, f32), j...  1.44 us

profile of v5, /device:TPU:0, one launch (start us, length us, event | category | flops | bytes accessed | tf_op | source)
XLA Modules:
  0.0 23.7 jit_solution(10720744448518039484)
XLA Ops:
  0.6 0.0 copy-start.2
  0.6 0.0 copy-start.1
  0.7 0.0 copy-start
  0.7 21.5 %shard_map.68 = (f32[68,80,128]{2,1,0:T(8,128)S(1)}, f32[68,80,128]{2,1,0:T(8,128)S(1)}, f32[68,80,128]{2,1,0:T(8,128)S(1)}, f32[8,128]{1,0:T(8,128)S(1)}, f32[2,3,16,128]{3,2,1,0:T(8,128)S(1)}) custom-call(f32[64,64,128]{2,1,0:T(8,128)} %load.1, f32[64,64,128]{2,1,0:T(8,128)} %stiff.1), custom_call_target="tpu_custom_call" | custom-call | tf_op jit(solution)/shard_map/pallas_call | solution.py:619
  22.2 0.0 copy-done.2
  22.2 0.0 copy-done.1
  22.2 0.0 copy-done
  22.2 1.4 %shard_map.69 = (f32[64,64,128]{2,1,0:T(8,128)}, f32[16,128]{1,0:T(8,128)}) custom-call(f32[68,80,128]{2,1,0:T(8,128)S(1)} %get-tuple-element.7.u0, f32[68,80,128]{2,1,0:T(8,128)S(1)} %get-tuple-element.8.u1, f32[68,80,128]{2,1,0:T(8,128)S(1)} %get-tuple-element.9.u2, f32[8,128]{1,0:T(8,128)S(1)} %get-tuple-element.10.coef_ref, ...), custom_call_target="tpu_custom_call" | custom-call | tf_op jit(solution)/shard_map/pallas_call | solution.py:660
Async XLA Ops:
  0.6 21.6 %copy-start.2 = (f32[16,128]{1,0:T(8,128)S(1)}, f32[16,128]{1,0:T(8,128)}, u32[]{:S(2)}) copy-start(f32[16,128]{1,0:T(8,128)} %norm_ref.1) | copy-start | bytes 24580
  0.6 21.6 %copy-start.1 = (f32[16,128]{1,0:T(8,128)S(1)}, f32[16,128]{1,0:T(8,128)}, u32[]{:S(2)}) copy-start(f32[16,128]{1,0:T(8,128)} %state_ref.1) | copy-start | bytes 24580
  0.7 21.6 %copy-start = (f32[16,128]{1,0:T(8,128)S(1)}, f32[16,128]{1,0:T(8,128)}, u32[]{:S(2)}) copy-start(f32[16,128]{1,0:T(8,128)} %pre_ref.1) | copy-start | bytes 24580
